TPU v7x, 512 devices: a whole 4x4x16 slice. The times are simulated.
512 devices in a mesh: wide: 32 (over z, x_hi), narrow: 16 (over y, x_lo, core).
Axes of the slice: x: 4 (x_hi: 2, x_lo: 2; x = x_hi * 2 + x_lo), y: 4, z: 16, core: 2. Of those that a mesh axis runs over, the one named last changes fastest.
Arguments:
- moments: float32 [16384, 2048], P('wide', 'narrow'), as said below
- eigen_basis: float32 [16384, 2048], P('wide', 'narrow'), may hold values from -0.125 to 0.125
- slot_order: int32 [8], replicated, may hold values 0 or 1
Outputs:
- halves: float32 [16384, 1024], P('wide', 'narrow')
Inputs may be any that keep to these rules, and one draw needn't show every extreme that they name: Each block of 2048 rows of moments is symmetric.
All inputs are finite; a program needn't handle non-finite values.
Results may differ from a plain program's by a relative error of at most 0.0001.
Values sent between devices are 32-bit elements; how exact they have to be, the bound alone decides.
No kernel may reach another device: no remote copies, remote signals or barrier semaphores. Data moves between devices by JAX's collectives and lax.ppermute only.
A program may use at most 64 MiB of HBM per device.

v0:
```python
import jax
import jax.numpy as jnp
from jax import lax
from jax.sharding import Mesh
from jax.sharding import PartitionSpec as P

GROUP_WIDE = 4
K = 1024
NARROW = ("narrow_0", "narrow_1", "narrow_2")


def from_everyone(x, axis):
    devices = lax.axis_size(axis)
    return lax.all_to_all(jnp.broadcast_to(x[None], (devices, *x.shape)), axis, 0, 0, tiled=True)


def in_order(parts, dim):
    parts = jnp.moveaxis(parts, 0, dim)
    lengths = parts.shape
    return parts.reshape(*lengths[:dim], lengths[dim] * lengths[dim + 1], *lengths[dim + 2 :])


def whole_of(x, axes, dim):
    far, near = axes
    first = from_everyone(x, far)
    parts = jnp.swapaxes(from_everyone(first, near), 0, 1)
    return in_order(parts.reshape(-1, *x.shape), dim)


def partner(value, axis, stride):
    mask = 2**stride
    pairs = [(source, source ^ mask) for source in range(lax.axis_size(axis))]
    return lax.ppermute(value, axis, pairs)


def body(moments, eigen_basis, slot_order):
    wide_pos = lax.axis_index("wide")
    subproblem = wide_pos // GROUP_WIDE
    position = wide_pos % GROUP_WIDE
    swapped = lax.dynamic_index_in_dim(slot_order, subproblem, 0, keepdims=False)
    narrow_pos = lax.axis_index(NARROW)
    col_count = eigen_basis.shape[1]
    half_cols = col_count // 2
    full_basis = whole_of(eigen_basis, (("narrow_0", "narrow_1"), "narrow_2"), 1)
    first_half = lax.dynamic_slice_in_dim(full_basis, narrow_pos * half_cols, half_cols, 1)
    second_half = lax.dynamic_slice_in_dim(full_basis, K + narrow_pos * half_cols, half_cols, 1)
    local_panel = jnp.concatenate([first_half, second_half], axis=1)
    pair_block = partner(local_panel, "wide", 0)
    joined = jnp.where(
        position % 2 == 0,
        jnp.concatenate([local_panel, pair_block], axis=0),
        jnp.concatenate([pair_block, local_panel], axis=0),
    )
    quad_block = partner(joined, "wide", 1)
    col_panel = jnp.where(
        position // 2 % 2 == 0,
        jnp.concatenate([joined, quad_block], axis=0),
        jnp.concatenate([quad_block, joined], axis=0),
    )
    products = jnp.dot(
        lax.all_gather(moments, NARROW, axis=1, tiled=True),
        col_panel,
        precision=lax.Precision.HIGHEST,
        preferred_element_type=jnp.float32,
    )
    partials = []
    for slot_index in range(2):
        half_panel = products[:, slot_index * half_cols : (slot_index + 1) * half_cols]
        vectors_half = full_basis[:, slot_index * K : (slot_index + 1) * K]
        partials.append(
            lax.dot_general(
                vectors_half,
                half_panel,
                (((0,), (0,)), ((), ())),
                precision=lax.Precision.HIGHEST,
                preferred_element_type=jnp.float32,
            )
        )
    stacked = jnp.stack(partials)
    slot_pick = (position // 2 + swapped) % 2
    row_part = position % 2
    kept = lax.dynamic_index_in_dim(stacked, slot_pick, 0, keepdims=False)
    sent = lax.dynamic_index_in_dim(stacked, 1 - slot_pick, 0, keepdims=False)
    merged = kept + partner(sent, "wide", 1)
    own_rows = lax.dynamic_slice_in_dim(merged, row_part * (K // 2), K // 2, 0)
    away_rows = lax.dynamic_slice_in_dim(merged, (1 - row_part) * (K // 2), K // 2, 0)
    return own_rows + partner(away_rows, "wide", 0)


def solution(mesh):
    torus = Mesh(
        mesh.devices.reshape(mesh.shape["wide"], 4, 2, 2),
        ("wide", "narrow_0", "narrow_1", "narrow_2"),
    )
    return jax.shard_map(
        body,
        mesh=torus,
        in_specs=(P("wide", NARROW), P("wide", NARROW), P()),
        out_specs=P("wide", NARROW),
        check_vma=False,
    )
```

profile of v0, /device:TPU:130, one launch (start us, length us, event | category | flops | bytes accessed | tf_op | source)
XLA Modules:
  0.0 129.6 jit_solution(15821226326817037298)
XLA Ops:
  6.5 0.0 all-gather.2.cloned.1.call-start
  6.5 0.7 all-gather.2.cloned.1.call-update
  7.3 2.4 %broadcast_in_dim.4 = f32[8,512,128]{2,1,0:T(8,128)} broadcast(f32[512,128]{1,0:T(8,128)} %param.4), dimensions={1,2} | broadcast | bytes 2359296 | tf_op jit(solution)/shard_map/broadcast_in_dim | solution.py:14
  9.7 5.9 %all-to-all-start = ((f32[8,512,128]{2,1,0:T(8,128)}), f32[8,512,128]{2,1,0:T(8,128)S(1)}, u32[]{:S(2)}, u32[]{:S(2)}) async-start(f32[8,512,128]{2,1,0:T(8,128)} %broadcast_in_dim.4), calls=%async_computation | async-start | bytes 4194304 | tf_op jit(solution)/shard_map/all_to_all | solution.py:14
  15.6 31.0 %all-to-all-done = f32[8,512,128]{2,1,0:T(8,128)S(1)} async-done(((f32[8,512,128]{2,1,0:T(8,128)}), f32[8,512,128]{2,1,0:T(8,128)S(1)}, u32[]{:S(2)}, u32[]{:S(2)}) %all-to-all-start) | async-done | bytes 2097184 | tf_op jit(solution)/shard_map/all_to_all | solution.py:14
  46.6 1.2 copy.7
  47.8 0.3 broadcast_in_dim.5
  48.0 7.2 %all_to_all.10 = f32[2,8,512,128]{3,1,2,0:T(8,128)S(1)} all-to-all(f32[2,8,512,128]{3,1,2,0:T(8,128)S(1)} %broadcast_in_dim.5), channel_id=1, replica_groups=mesh['wide'=32,'narrow_0'=4,'narrow_1'=2,'narrow_2'=2] {'narrow_2'}, dimensions={0} | all-to-all | bytes 8388608 | tf_op jit(solution)/shard_map/all_to_all | solution.py:14
  55.2 2.7 %copy.8 = f32[2,8,512,128]{3,2,0,1:T(8,128)} copy(f32[2,8,512,128]{3,1,2,0:T(8,128)S(1)} %all_to_all.10) | data formatting | bytes 8388608 | tf_op jit(solution)/shard_map/all_to_all | solution.py:14
  58.0 0.0 copy-start.1
  58.0 5.4 %copy.9 = f32[512,16,128]{0,2,1:T(8,128)} copy(f32[512,16,128]{2,0,1:T(8,128)} %bitcast.27) | data formatting | bytes 8388608 | tf_op jit(solution)/shard_map/transpose | solution.py:18
  63.4 1.0 constant_dynamic-slice_fusion.2
  64.4 4.0 %collective-permute-start = (f32[512,128]{0,1:T(8,128)S(1)}, f32[512,128]{0,1:T(8,128)S(1)}, u32[]{:S(2)}, u32[]{:S(2)}) collective-permute-start(f32[512,128]{0,1:T(8,128)S(1)} %pad_maximum_fusion), channel_id=1, source_target_pairs={{0,16},{16,0},{32,48},{48,32},{64,80},{80,64},{96,112},{112,96},{1... | collective-permute-start | bytes 786440 | tf_op jit(solution)/shard_map/ppermute | solution.py:33
  68.5 9.2 %collective-permute-done = f32[512,128]{0,1:T(8,128)S(1)} collective-permute-done((f32[512,128]{0,1:T(8,128)S(1)}, f32[512,128]{0,1:T(8,128)S(1)}, u32[]{:S(2)}, u32[]{:S(2)}) %collective-permute-start) | collective-permute-done | bytes 262176 | tf_op jit(solution)/shard_map/ppermute | solution.py:33
  77.7 3.8 %collective-permute-start.1 = (f32[1024,128]{0,1:T(8,128)S(1)}, f32[1024,128]{0,1:T(8,128)S(1)}, u32[]{:S(2)}, u32[]{:S(2)}) collective-permute-start(f32[1024,128]{0,1:T(8,128)S(1)} %maximum_select_fusion.2), channel_id=1, source_target_pairs={{0,32},{16,48},{32,0},{48,16},{64,96},{80,112},{96,64},{112,80},{1... | collective-permute-start | bytes 1572872 | tf_op jit(solution)/shard_map/ppermute | solution.py:33
  81.6 0.0 copy-done.1
  81.6 0.6 dynamic_slice.25
  82.9 10.5 %collective-permute-done.1 = f32[1024,128]{0,1:T(8,128)S(1)} collective-permute-done((f32[1024,128]{0,1:T(8,128)S(1)}, f32[1024,128]{0,1:T(8,128)S(1)}, u32[]{:S(2)}, u32[]{:S(2)}) %collective-permute-start.1) | collective-permute-done | bytes 524320 | tf_op jit(solution)/shard_map/ppermute | solution.py:33
  93.4 0.0 all-gather.2.cloned.1.call-done
  93.4 0.0 copy-start
  93.4 6.6 %convolution_bitcast_fusion = f32[512,128]{0,1:T(8,128)S(1)} fusion(f32[512,2048]{1,0:T(8,128)} %all-gather.2.cloned.1.call-done, f32[1024,128]{0,1:T(8,128)S(1)} %collective-permute-done.1, f32[1024,128]{0,1:T(8,128)S(1)} %maximum_select_fusion.2, pred[]{:T(512)S(6)} %eq.12), kind=kOutput, calls=%fused_computation.4 | convolution fusion | flops 1611399168 | bytes 5505025 | tf_op jit(solution)/shard_map/dot_general | solution.py:60
  100.1 0.0 copy-done
  100.1 2.1 %fusion.4 = f32[1,1024,64]{1,2,0:T(8,128)S(1)} fusion(f32[512,2048]{0,1:T(8,128)S(1)} %bitcast.25, f32[512,128]{0,1:T(8,128)S(1)} %convolution_bitcast_fusion), kind=kOutput, calls=%fused_computation.5 | convolution fusion | flops 402653184 | bytes 2490368 | tf_op jit(solution)/shard_map/dot_general | solution.py:71
  102.2 2.1 %fusion.7 = f32[1,1024,64]{1,2,0:T(8,128)S(1)} fusion(f32[512,2048]{0,1:T(8,128)S(1)} %bitcast.26, f32[512,128]{0,1:T(8,128)S(1)} %convolution_bitcast_fusion), kind=kOutput, calls=%fused_computation.6 | convolution fusion | flops 402653184 | bytes 2490368 | tf_op jit(solution)/shard_map/dot_general | solution.py:71
  104.4 0.1 fusion.17
  104.4 3.6 %collective-permute-start.2 = (f32[1024,64]{0,1:T(8,128)S(1)}, f32[1024,64]{0,1:T(8,128)S(1)}, u32[]{:S(2)}, u32[]{:S(2)}) collective-permute-start(f32[1024,64]{0,1:T(8,128)S(1)} %fusion.17), channel_id=1, source_target_pairs={{0,32},{16,48},{32,0},{48,16},{64,96},{80,112},{96,64},{112,80},{1... | collective-permute-start | bytes 786440 | tf_op jit(solution)/shard_map/ppermute | solution.py:33
  108.1 5.6 %collective-permute-done.2 = f32[1024,64]{0,1:T(8,128)S(1)} collective-permute-done((f32[1024,64]{0,1:T(8,128)S(1)}, f32[1024,64]{0,1:T(8,128)S(1)}, u32[]{:S(2)}, u32[]{:S(2)}) %collective-permute-start.2) | collective-permute-done | bytes 262176 | tf_op jit(solution)/shard_map/ppermute | solution.py:33
  113.6 0.1 fusion.20
  113.7 3.2 %collective-permute-start.3 = (f32[512,64]{0,1:T(8,128)S(1)}, f32[512,64]{0,1:T(8,128)S(1)}, u32[]{:S(2)}, u32[]{:S(2)}) collective-permute-start(f32[512,64]{0,1:T(8,128)S(1)} %constant_dynamic-slice_fusion), channel_id=1, source_target_pairs={{0,16},{16,0},{32,48},{48,32},{64,80},{80,64},{96,112},{112,96},{1... | collective-permute-start | bytes 393224 | tf_op jit(solution)/shard_map/ppermute | solution.py:33
  117.0 5.1 %collective-permute-done.3 = f32[512,64]{0,1:T(8,128)S(1)} collective-permute-done((f32[512,64]{0,1:T(8,128)S(1)}, f32[512,64]{0,1:T(8,128)S(1)}, u32[]{:S(2)}, u32[]{:S(2)}) %collective-permute-start.3) | collective-permute-done | bytes 131104 | tf_op jit(solution)/shard_map/ppermute | solution.py:33
  122.1 0.7 dynamic-slice_add_fusion
  (3 shorter events, 0.1 us)
Async XLA Ops:
  6.5 86.9 %all-gather.2.cloned.1.call-start = ((), (), s32[]{:S(2)}) async-start(), calls=%async_computation.2 | async-start | bytes 4456448 | tf_op jit(solution)/shard_map/all_gather | solution.py:61
  9.7 36.9 %all-to-all-start = ((f32[8,512,128]{2,1,0:T(8,128)}), f32[8,512,128]{2,1,0:T(8,128)S(1)}, u32[]{:S(2)}, u32[]{:S(2)}) async-start(f32[8,512,128]{2,1,0:T(8,128)} %broadcast_in_dim.4), calls=%async_computation | async-start | bytes 4194304 | tf_op jit(solution)/shard_map/all_to_all | solution.py:14
  58.0 23.6 %copy-start.1 = (s32[8]{0:T(128)S(1)}, s32[8]{0:T(128)}, u32[]{:S(2)}) copy-start(s32[8]{0:T(128)} %param.5) | copy-start | bytes 100
  64.4 13.3 %collective-permute-start = (f32[512,128]{0,1:T(8,128)S(1)}, f32[512,128]{0,1:T(8,128)S(1)}, u32[]{:S(2)}, u32[]{:S(2)}) collective-permute-start(f32[512,128]{0,1:T(8,128)S(1)} %pad_maximum_fusion), channel_id=1, source_target_pairs={{0,16},{16,0},{32,48},{48,32},{64,80},{80,64},{96,112},{112,96},{1... | collective-permute-start | bytes 786440 | tf_op jit(solution)/shard_map/ppermute | solution.py:33
  77.7 15.7 %collective-permute-start.1 = (f32[1024,128]{0,1:T(8,128)S(1)}, f32[1024,128]{0,1:T(8,128)S(1)}, u32[]{:S(2)}, u32[]{:S(2)}) collective-permute-start(f32[1024,128]{0,1:T(8,128)S(1)} %maximum_select_fusion.2), channel_id=1, source_target_pairs={{0,32},{16,48},{32,0},{48,16},{64,96},{80,112},{96,64},{112,80},{1... | collective-permute-start | bytes 1572872 | tf_op jit(solution)/shard_map/ppermute | solution.py:33
  93.4 6.7 %copy-start = (f32[512,16,128]{0,2,1:T(8,128)S(1)}, f32[512,16,128]{0,2,1:T(8,128)}, u32[]{:S(2)}) copy-start(f32[512,16,128]{0,2,1:T(8,128)} %copy.9) | copy-start | bytes 12582916
  104.4 9.2 %collective-permute-start.2 = (f32[1024,64]{0,1:T(8,128)S(1)}, f32[1024,64]{0,1:T(8,128)S(1)}, u32[]{:S(2)}, u32[]{:S(2)}) collective-permute-start(f32[1024,64]{0,1:T(8,128)S(1)} %fusion.17), channel_id=1, source_target_pairs={{0,32},{16,48},{32,0},{48,16},{64,96},{80,112},{96,64},{112,80},{1... | collective-permute-start | bytes 786440 | tf_op jit(solution)/shard_map/ppermute | solution.py:33
  113.7 8.4 %collective-permute-start.3 = (f32[512,64]{0,1:T(8,128)S(1)}, f32[512,64]{0,1:T(8,128)S(1)}, u32[]{:S(2)}, u32[]{:S(2)}) collective-permute-start(f32[512,64]{0,1:T(8,128)S(1)} %constant_dynamic-slice_fusion), channel_id=1, source_target_pairs={{0,16},{16,0},{32,48},{48,32},{64,80},{80,64},{96,112},{112,96},{1... | collective-permute-start | bytes 393224 | tf_op jit(solution)/shard_map/ppermute | solution.py:33
Sparse Core Ops, SparseCore 0:
  9.4 61.0 all-gather.1
where the time goes:
time: 130 us
  waiting for transfers between devices  62 us (48%)
  starting transfers between devices  20.7 us (16%)
  between operations  14.3 us (11%)
  local copies, waits for them, and re-layouts  13.6 us (10%)
  matrix products  10.9 us (8%)
  blocking collectives  7.19 us (6%)
    all_to_all x1, waiting for transfers between devices, from_everyone(): lax.all_to_all(jnp.broadcast_to(x[None], (devices, *x.shape)), axis, 0, 0...  31 us
    ppermute x4, waiting for transfers between devices, partner(): return lax.ppermute(value, axis, pairs)  30.4 us
    ppermute x4, starting transfers between devices, partner(): return lax.ppermute(value, axis, pairs)  14.7 us
    all_to_all x1, blocking collectives, from_everyone(): lax.all_to_all(jnp.broadcast_to(x[None], (devices, *x.shape)), axis, 0, 0...  7.19 us
    dot_general x1, matrix products, body(): jnp.dot(lax.all_gather(moments, NARROW, axis=1, tiled=True), col_panel, p...  6.64 us
    all_to_all x1, starting transfers between devices, from_everyone(): lax.all_to_all(jnp.broadcast_to(x[None], (devices, *x.shape)), axis, 0, 0...  5.93 us
    transpose x1, local copies, waits for them, and re-layouts, in_order(): parts = jnp.moveaxis(parts, 0, dim)  5.43 us
    dot_general x2, matrix products, body(): lax.dot_general(vectors_half, half_panel, (((0,), (0,)), ((), ())), preci...  4.28 us
  transfers between devices with their start and end apart: 6, of which 5 were waited for; matrix products, arithmetic and copies ran while one was open for 11% of the time, Pallas kernels for 0%

commit v1 on v0

v1 whole, which is shorter than its diff:
```python
import functools

import jax
import jax.numpy as jnp
from jax import lax
from jax.experimental import pallas as pl
from jax.experimental.pallas import tpu as pltpu
from jax.sharding import Mesh
from jax.sharding import PartitionSpec as P

ROW = ("zl", "xh")
COL = ("y", "xl", "c")


def split(x):
    high = x.astype(jnp.bfloat16)
    return high, (x - high.astype(jnp.float32)).astype(jnp.bfloat16)


def product(left, right, dims):
    left_high, left_low = left
    right_high, right_low = right
    dot = functools.partial(lax.dot_general, dimension_numbers=(dims, ((), ())), preferred_element_type=jnp.float32)
    return dot(left_high, right_high) + (dot(left_high, right_low) + dot(left_low, right_high))


def image_kernel(swap_ref, a_ref, v_ref, z_ref):
    swap = swap_ref[0]
    rows = [split(a_ref[part]) for part in range(4)]
    for slot in range(2):
        for block in range(2):
            cols = split(v_ref[(slot ^ swap) * 2 + block])
            for part in range(4):
                z_ref[slot * 2 + block, part * 128 : (part + 1) * 128, :] = product(rows[part], cols, ((0,), (0,)))


def image(swap, a, v):
    return pl.pallas_call(
        image_kernel,
        out_shape=jax.ShapeDtypeStruct((4, 512, 128), jnp.float32),
        in_specs=[pl.BlockSpec(memory_space=pltpu.SMEM)] + [pl.BlockSpec(memory_space=pltpu.VMEM)] * 2,
        out_specs=pl.BlockSpec(memory_space=pltpu.VMEM),
        cost_estimate=pl.CostEstimate(flops=6 * 512**3, bytes_accessed=3 * 2**20, transcendentals=0),
    )(swap, a, v)


def project_kernel(half_ref, v_ref, *refs):
    z_refs, y_ref = refs[:-1], refs[-1]
    half = half_ref[0]
    pieces = len(z_refs)
    depth = 512 // pieces
    for block in range(2):
        rows = split(v_ref[half * 2 + block])
        for part in range(4):
            total = None
            for piece in range(pieces):
                cut = slice(piece * depth, (piece + 1) * depth)
                term = product((rows[0][:, cut], rows[1][:, cut]), split(z_refs[piece][part]), ((1,), (0,)))
                total = term if total is None else total + term
            y_ref[block * 2, :, part * 128 : (part + 1) * 128] = total[:64]
            y_ref[block * 2 + 1, :, part * 128 : (part + 1) * 128] = total[64:]


def project(half, v, z):
    return pl.pallas_call(
        project_kernel,
        out_shape=jax.ShapeDtypeStruct((4, 64, 512), jnp.float32),
        in_specs=[pl.BlockSpec(memory_space=pltpu.SMEM)] + [pl.BlockSpec(memory_space=pltpu.VMEM)] * (1 + len(z)),
        out_specs=pl.BlockSpec(memory_space=pltpu.VMEM),
        cost_estimate=pl.CostEstimate(flops=3 * 512**3, bytes_accessed=2 * 2**20, transcendentals=0),
    )(half, v, *z)


def exchange(x, axes):
    return lax.all_to_all(x, axes, 0, 0, tiled=True)


def pair(x, axis):
    other = lax.ppermute(x, axis, [(0, 1), (1, 0)])
    first = lax.axis_index(axis) == 0
    return jnp.where(first, jnp.stack([x, other]), jnp.stack([other, x]))


def body(moments, basis, slot_order):
    swap = lax.dynamic_slice_in_dim(slot_order, lax.axis_index("g"), 1)
    half = lax.axis_index("zl").astype(jnp.int32) ^ swap
    basis_y = exchange(jnp.broadcast_to(basis, (4, 512, 128)), "y")
    moments_q = jnp.swapaxes(pair(pair(moments, "xl"), "c"), 0, 1).reshape(4, 512, 128)

    turned = basis.T.reshape(2, 64, 512)
    x_pos = lax.axis_index("xl")
    c_pos = lax.axis_index("c")
    got = []
    for step in range(2):
        routes = [(x * 2 + c, c * 2 + (x ^ step)) for x in range(2) for c in range(2)]
        got.append(lax.ppermute(lax.dynamic_index_in_dim(turned, x_pos ^ step, 0, keepdims=False), ("xl", "c"), routes))
    mixed = jnp.where(c_pos == 0, jnp.concatenate(got, 0), jnp.concatenate(got[::-1], 0))
    basis_rows = exchange(exchange(jnp.broadcast_to(mixed, (4, 128, 512)), ROW), "y")

    partial = exchange(image(swap, moments_q, basis_y), ROW)
    total = (partial[0] + partial[1]) + (partial[2] + partial[3])
    z = [lax.all_gather(total[i * 256 : (i + 1) * 256], ("xl", "c"), axis=0) for i in range(2)]
    out = exchange(project(half, basis_rows, z), "y")
    return ((out[0] + out[1]) + (out[2] + out[3])).T


def solution(mesh):
    torus = Mesh(mesh.devices.reshape(mesh.shape["wide"] // 4, 2, 2, 4, 2, 2), ("g", *ROW, *COL))
    spec = P(("g", *ROW), COL)
    return jax.shard_map(body, mesh=torus, in_specs=(spec, spec, P()), out_specs=spec, check_vma=False)
```

time: 130 us -> 116 us (0.89)
  the two profiles are of different devices: /device:TPU:130 before, /device:TPU:352 now
where the time goes in v1:
time: 116 us; the launch traced here: 115 us
  waiting for transfers between devices  38.7 us (33%)
  starting transfers between devices  30.6 us (26%)
  blocking collectives  29.3 us (25%)
  Pallas kernels  8.32 us (7%)
  local copies, waits for them, and re-layouts  6.84 us (6%)
    all_to_all x4, waiting for transfers between devices, exchange(): return lax.all_to_all(x, axes, 0, 0, tiled=True)  21.2 us
    all_to_all x4, starting transfers between devices, exchange(): return lax.all_to_all(x, axes, 0, 0, tiled=True)  20.4 us
    all_gather x2, blocking collectives, body(): lax.all_gather(total[i * 256:(i + 1) * 256], ('xl', 'c'), axis=0)  15.1 us
    ppermute x2, waiting for transfers between devices, pair(): other = lax.ppermute(x, axis, [(0, 1), (1, 0)])  14.7 us
    all_to_all x1, blocking collectives, exchange(): return lax.all_to_all(x, axes, 0, 0, tiled=True)  14.1 us
    ppermute x2, starting transfers between devices, body(): lax.ppermute(lax.dynamic_index_in_dim(turned, x_pos ^ step, 0, keepdims=F...  5.42 us
    pallas_call x1, Pallas kernels, image(): pl.pallas_call(image_kernel, out_shape=jax.ShapeDtypeStruct((4, 512, 128)...  5.02 us
    ppermute x2, starting transfers between devices, pair(): other = lax.ppermute(x, axis, [(0, 1), (1, 0)])  4.78 us
  transfers between devices with their start and end apart: 8, of which 6 were waited for; matrix products, arithmetic and copies ran while one was open for 2% of the time, Pallas kernels for 4%

profile of v1, /device:TPU:352, one launch (start us, length us, event | category | flops | bytes accessed | tf_op | source)
XLA Modules:
  0.0 115.4 jit_solution(3370335603745752213)
XLA Ops:
  0.0 2.0 %broadcast_in_dim.7 = f32[4,512,128]{2,1,0:T(8,128)} broadcast(f32[512,128]{1,0:T(8,128)} %param.4), dimensions={1,2} | broadcast | bytes 1310720 | tf_op jit(solution)/shard_map/broadcast_in_dim | solution.py:87
  2.0 0.0 copy-start.2
  2.0 4.6 %all-to-all-start.2 = ((f32[4,512,128]{2,1,0:T(8,128)}), f32[4,512,128]{2,1,0:T(8,128)S(1)}, u32[]{:S(2)}, u32[]{:S(2)}) async-start(f32[4,512,128]{2,1,0:T(8,128)} %broadcast_in_dim.7), calls=%async_computation.2 | async-start | bytes 2097152 | tf_op jit(solution)/shard_map/all_to_all | solution.py:75
  6.6 0.0 copy-done.2
  6.6 0.1 copy.9
  6.8 0.7 collective-permute-start
  7.5 4.8 %collective-permute-start.1 = (f32[64,512]{1,0:T(8,128)S(1)}, f32[64,512]{1,0:T(8,128)S(1)}, u32[]{:S(2)}, u32[]{:S(2)}) collective-permute-start(f32[64,512]{1,0:T(8,128)S(1)} %get-tuple-element.8), channel_id=1, source_target_pairs={{0,1},{1,3},{2,0},{3,2},{4,5},{5,7},{6,4},{7,6},{8,9},{9,11},{10,8... | collective-permute-start | bytes 393224 | tf_op jit(solution)/shard_map/ppermute | solution.py:96
  12.2 0.0 collective-permute-done
  12.2 2.8 %collective-permute-done.1 = f32[64,512]{1,0:T(8,128)S(1)} collective-permute-done((f32[64,512]{1,0:T(8,128)S(1)}, f32[64,512]{1,0:T(8,128)S(1)}, u32[]{:S(2)}, u32[]{:S(2)}) %collective-permute-start.1) | collective-permute-done | bytes 131104 | tf_op jit(solution)/shard_map/ppermute | solution.py:96
  15.1 6.6 %all-to-all-done.2.v_ref = f32[4,512,128]{2,1,0:T(8,128)S(1)} async-done(((f32[4,512,128]{2,1,0:T(8,128)}), f32[4,512,128]{2,1,0:T(8,128)S(1)}, u32[]{:S(2)}, u32[]{:S(2)}) %all-to-all-start.2) | async-done | bytes 1048608 | tf_op jit(solution)/shard_map/all_to_all | solution.py:75
  21.7 0.0 copy-start
  21.7 1.3 %broadcast_in_dim.6 = f32[4,128,512]{2,1,0:T(8,128)} broadcast(f32[128,512]{1,0:T(8,128)S(1)} %maximum_select_fusion.3), dimensions={1,2} | broadcast | bytes 1310720 | tf_op jit(solution)/shard_map/broadcast_in_dim | solution.py:98
  23.0 0.0 copy-start.3
  23.0 0.1 copy-done
  23.0 5.8 %all-to-all-start = ((f32[4,128,512]{2,1,0:T(8,128)}), f32[4,128,512]{2,1,0:T(8,128)}, u32[]{:S(2)}, u32[]{:S(2)}) async-start(f32[4,128,512]{2,1,0:T(8,128)} %broadcast_in_dim.6), calls=%async_computation | async-start | bytes 2097152 | tf_op jit(solution)/shard_map/all_to_all | solution.py:75
  28.8 0.0 copy-done.3
  28.8 2.9 %collective-permute-start.2 = (f32[512,128]{1,0:T(8,128)S(1)}, f32[512,128]{1,0:T(8,128)S(1)}, u32[]{:S(2)}, u32[]{:S(2)}) collective-permute-start(f32[512,128]{1,0:T(8,128)S(1)} %copy-done.3), channel_id=1, source_target_pairs={{0,2},{2,0},{1,3},{3,1},{4,6},{6,4},{5,7},{7,5},{8,10},{10,8},{9,1... | collective-permute-start | bytes 786440 | tf_op jit(solution)/shard_map/ppermute | solution.py:79
  31.7 14.2 %collective-permute-done.2 = f32[512,128]{1,0:T(8,128)S(1)} collective-permute-done((f32[512,128]{1,0:T(8,128)S(1)}, f32[512,128]{1,0:T(8,128)S(1)}, u32[]{:S(2)}, u32[]{:S(2)}) %collective-permute-start.2) | collective-permute-done | bytes 262176 | tf_op jit(solution)/shard_map/ppermute | solution.py:79
  45.9 1.9 %collective-permute-start.3 = (f32[2,512,128]{2,1,0:T(8,128)S(1)}, f32[2,512,128]{2,1,0:T(8,128)S(1)}, u32[]{:S(2)}, u32[]{:S(2)}) collective-permute-start(f32[2,512,128]{2,1,0:T(8,128)S(1)} %maximum_select_fusion.2), channel_id=1, source_target_pairs={{0,1},{1,0},{2,3},{3,2},{4,5},{5,4},{6,7},{7,6},{8,9},{9,8},{10,11... | collective-permute-start | bytes 1572872 | tf_op jit(solution)/shard_map/ppermute | solution.py:79
  47.8 0.0 copy-start.4
  47.8 0.6 copy-done.4
  48.5 0.6 dynamic_slice.10.swap_ref
  49.1 0.5 collective-permute-done.3
  49.7 0.1 fusion
  49.7 1.0 copy.10
  50.8 5.0 %shard_map.37 = f32[4,512,128]{2,1,0:T(8,128)} custom-call(s32[1]{0:T(128)} %dynamic_slice.10.swap_ref, f32[4,512,128]{2,1,0:T(8,128)} %bitcast.20, f32[4,512,128]{2,1,0:T(8,128)} %copy-done), custom_call_target="tpu_custom_call" | custom-call | flops 805306368 | bytes 3145728 | tf_op jit(solution)/shard_map/pallas_call | solution.py:38
  55.8 0.0 all-to-all-done
  55.8 6.5 %all-to-all-start.3 = ((f32[4,512,128]{2,1,0:T(8,128)}), f32[4,512,128]{2,1,0:T(8,128)S(1)}, u32[]{:S(2)}, u32[]{:S(2)}) async-start(f32[4,512,128]{2,1,0:T(8,128)} %shard_map.37), calls=%async_computation.3 | async-start | bytes 2097152 | tf_op jit(solution)/shard_map/all_to_all | solution.py:75
  63.0 14.2 %all-to-all-done.3 = f32[4,512,128]{2,1,0:T(8,128)S(1)} async-done(((f32[4,512,128]{2,1,0:T(8,128)}), f32[4,512,128]{2,1,0:T(8,128)S(1)}, u32[]{:S(2)}, u32[]{:S(2)}) %all-to-all-start.3) | async-done | bytes 1048608 | tf_op jit(solution)/shard_map/all_to_all | solution.py:75
  77.2 3.5 %all-to-all-start.1 = ((f32[4,128,512]{2,1,0:T(8,128)}), f32[4,128,512]{2,1,0:T(8,128)S(1)}, u32[]{:S(2)}, u32[]{:S(2)}) async-start(f32[4,128,512]{2,1,0:T(8,128)} %all-to-all-done), calls=%async_computation.1 | async-start | bytes 2097152 | tf_op jit(solution)/shard_map/all_to_all | solution.py:75
  80.7 0.1 fusion.1
  80.8 7.4 %all_gather.9.refs_1_ = f32[4,256,128]{2,1,0:T(8,128)} all-gather(f32[1,256,128]{2,1,0:T(8,128)S(1)} %get-tuple-element.5), channel_id=1, replica_groups=mesh['g'=8,'zl'=2,'xh'=2,'y'=4,'xl'=2,'c'=2] {'xl','c'}, dimensions={0}, use_global_device_ids=true | all-gather | bytes 655360 | tf_op jit(solution)/shard_map/all_gather | solution.py:102
  88.2 7.7 %all_gather.8.refs_0_ = f32[4,256,128]{2,1,0:T(8,128)} all-gather(f32[1,256,128]{2,1,0:T(8,128)S(1)} %get-tuple-element.6), channel_id=1, replica_groups=mesh['g'=8,'zl'=2,'xh'=2,'y'=4,'xl'=2,'c'=2] {'xl','c'}, dimensions={0}, use_global_device_ids=true | all-gather | bytes 655360 | tf_op jit(solution)/shard_map/all_gather | solution.py:102
  95.9 0.3 all-to-all-done.1.v_ref
  96.2 0.0 copy-start.1
  96.2 1.0 copy-done.1
  97.2 3.3 %shard_map.38 = f32[4,64,512]{2,1,0:T(8,128)} custom-call(s32[1]{0:T(128)S(6)} %xor.10.half_ref, f32[4,128,512]{2,1,0:T(8,128)} %copy-done.1, f32[4,256,128]{2,1,0:T(8,128)} %all_gather.8.refs_0_, f32[4,256,128]{2,1,0:T(8,128)} %all_gather.9.refs_1_), custom_call_target="tpu_custom_call" | custom-call | flops 402653184 | bytes 2097152 | tf_op jit(solution)/shard_map/pallas_call | solution.py:65
  100.5 14.1 %all_to_all.25 = f32[4,64,512]{2,1,0:T(8,128)S(1)} all-to-all(f32[4,64,512]{2,1,0:T(8,128)} %shard_map.38), channel_id=1, replica_groups=mesh['g'=8,'zl'=2,'xh'=2,'y'=4,'xl'=2,'c'=2] {'y'}, dimensions={0} | all-to-all | bytes 1048576 | tf_op jit(solution)/shard_map/all_to_all | solution.py:75
  114.7 0.7 fusion.3
  (5 shorter events, 0.1 us)
Async XLA Ops:
  2.0 4.6 %copy-start.2 = (f32[512,128]{1,0:T(8,128)S(1)}, f32[512,128]{1,0:T(8,128)}, u32[]{:S(2)}) copy-start(f32[512,128]{1,0:T(8,128)} %param.4) | copy-start | bytes 786436
  2.0 19.7 %all-to-all-start.2 = ((f32[4,512,128]{2,1,0:T(8,128)}), f32[4,512,128]{2,1,0:T(8,128)S(1)}, u32[]{:S(2)}, u32[]{:S(2)}) async-start(f32[4,512,128]{2,1,0:T(8,128)} %broadcast_in_dim.7), calls=%async_computation.2 | async-start | bytes 2097152 | tf_op jit(solution)/shard_map/all_to_all | solution.py:75
  6.8 5.4 %collective-permute-start = (f32[64,512]{1,0:T(8,128)S(1)}, f32[64,512]{1,0:T(8,128)S(1)}, u32[]{:S(2)}, u32[]{:S(2)}) collective-permute-start(f32[64,512]{1,0:T(8,128)S(1)} %get-tuple-element.7), channel_id=1, source_target_pairs={{0,0},{1,2},{2,1},{3,3},{4,4},{5,6},{6,5},{7,7},{8,8},{9,10},{10,9... | collective-permute-start | bytes 393224 | tf_op jit(solution)/shard_map/ppermute | solution.py:96
  7.5 7.6 %collective-permute-start.1 = (f32[64,512]{1,0:T(8,128)S(1)}, f32[64,512]{1,0:T(8,128)S(1)}, u32[]{:S(2)}, u32[]{:S(2)}) collective-permute-start(f32[64,512]{1,0:T(8,128)S(1)} %get-tuple-element.8), channel_id=1, source_target_pairs={{0,1},{1,3},{2,0},{3,2},{4,5},{5,7},{6,4},{7,6},{8,9},{9,11},{10,8... | collective-permute-start | bytes 393224 | tf_op jit(solution)/shard_map/ppermute | solution.py:96
  21.7 1.4 %copy-start = (f32[4,512,128]{2,1,0:T(8,128)}, f32[4,512,128]{2,1,0:T(8,128)S(1)}, u32[]{:S(2)}) copy-start(f32[4,512,128]{2,1,0:T(8,128)S(1)} %all-to-all-done.2.v_ref) | copy-start | bytes 3145732
  23.0 5.8 %copy-start.3 = (f32[512,128]{1,0:T(8,128)S(1)}, f32[512,128]{1,0:T(8,128)}, u32[]{:S(2)}) copy-start(f32[512,128]{1,0:T(8,128)} %param.3) | copy-start | bytes 786436
  23.0 32.8 %all-to-all-start = ((f32[4,128,512]{2,1,0:T(8,128)}), f32[4,128,512]{2,1,0:T(8,128)}, u32[]{:S(2)}, u32[]{:S(2)}) async-start(f32[4,128,512]{2,1,0:T(8,128)} %broadcast_in_dim.6), calls=%async_computation | async-start | bytes 2097152 | tf_op jit(solution)/shard_map/all_to_all | solution.py:75
  28.8 17.0 %collective-permute-start.2 = (f32[512,128]{1,0:T(8,128)S(1)}, f32[512,128]{1,0:T(8,128)S(1)}, u32[]{:S(2)}, u32[]{:S(2)}) collective-permute-start(f32[512,128]{1,0:T(8,128)S(1)} %copy-done.3), channel_id=1, source_target_pairs={{0,2},{2,0},{1,3},{3,1},{4,6},{6,4},{5,7},{7,5},{8,10},{10,8},{9,1... | collective-permute-start | bytes 786440 | tf_op jit(solution)/shard_map/ppermute | solution.py:79
  45.9 3.8 %collective-permute-start.3 = (f32[2,512,128]{2,1,0:T(8,128)S(1)}, f32[2,512,128]{2,1,0:T(8,128)S(1)}, u32[]{:S(2)}, u32[]{:S(2)}) collective-permute-start(f32[2,512,128]{2,1,0:T(8,128)S(1)} %maximum_select_fusion.2), channel_id=1, source_target_pairs={{0,1},{1,0},{2,3},{3,2},{4,5},{5,4},{6,7},{7,6},{8,9},{9,8},{10,11... | collective-permute-start | bytes 1572872 | tf_op jit(solution)/shard_map/ppermute | solution.py:79
  47.8 0.7 copy-start.4
  55.8 21.4 %all-to-all-start.3 = ((f32[4,512,128]{2,1,0:T(8,128)}), f32[4,512,128]{2,1,0:T(8,128)S(1)}, u32[]{:S(2)}, u32[]{:S(2)}) async-start(f32[4,512,128]{2,1,0:T(8,128)} %shard_map.37), calls=%async_computation.3 | async-start | bytes 2097152 | tf_op jit(solution)/shard_map/all_to_all | solution.py:75
  77.2 19.0 %all-to-all-start.1 = ((f32[4,128,512]{2,1,0:T(8,128)}), f32[4,128,512]{2,1,0:T(8,128)S(1)}, u32[]{:S(2)}, u32[]{:S(2)}) async-start(f32[4,128,512]{2,1,0:T(8,128)} %all-to-all-done), calls=%async_computation.1 | async-start | bytes 2097152 | tf_op jit(solution)/shard_map/all_to_all | solution.py:75
  96.2 1.0 copy-start.1

commit v2 on v1

v2 whole, which is shorter than its diff:
```python
import functools

import jax
import jax.numpy as jnp
from jax import lax
from jax.experimental import pallas as pl
from jax.experimental.pallas import tpu as pltpu
from jax.sharding import Mesh
from jax.sharding import PartitionSpec as P


ROW = ("zl", "xh")
COL = ("y", "xl", "c")


def split(x):
    high = x.astype(jnp.bfloat16)
    return high, (x - high.astype(jnp.float32)).astype(jnp.bfloat16)


def product(left, right, dims):
    left_high, left_low = left
    right_high, right_low = right
    dot = functools.partial(lax.dot_general, dimension_numbers=(dims, ((), ())), preferred_element_type=jnp.float32)
    return dot(left_high, right_high) + (dot(left_high, right_low) + dot(left_low, right_high))


SMALL = pltpu.CompilerParams(vmem_limit_bytes=24 * 2**20)
IN_VMEM = pl.BlockSpec(memory_space=pltpu.VMEM)
IN_SMEM = pl.BlockSpec(memory_space=pltpu.SMEM)


def image_kernel(place_ref, *refs):
    a_refs, v_ref, z_ref = refs[:4], refs[4], refs[5]
    swap, column = place_ref[0], place_ref[1]
    rows = [split(a_ref[...]) for a_ref in a_refs]
    for slot in range(2):
        for block in range(2):
            cols = split(v_ref[(slot ^ swap) * 2 + block])
            for part in range(4):
                start = pl.multiple_of((column ^ part) * 128, 128)
                z_ref[slot * 2 + block, pl.ds(start, 128), :] = product(rows[part], cols, ((0,), (0,)))


def image(place, a, v):
    return pl.pallas_call(
        image_kernel,
        out_shape=jax.ShapeDtypeStruct((4, 512, 128), jnp.float32),
        in_specs=[IN_SMEM] + [IN_VMEM] * 5,
        out_specs=IN_VMEM,
        compiler_params=SMALL,
        cost_estimate=pl.CostEstimate(flops=6 * 512**3, bytes_accessed=3 * 2**20, transcendentals=0),
    )(place, *a, v)


def project_kernel(half_ref, v_ref, *refs):
    z_refs, y_ref = refs[:-1], refs[-1]
    half = half_ref[0]
    depth = 512 // len(z_refs)
    for block in range(2):
        rows = split(v_ref[half * 2 + block])
        for part in range(4):
            total = None
            for piece, z_ref in enumerate(z_refs):
                cut = slice(piece * depth, (piece + 1) * depth)
                term = product((rows[0][:, cut], rows[1][:, cut]), split(z_ref[part]), ((1,), (0,)))
                total = term if total is None else total + term
            y_ref[block * 2, :, part * 128 : (part + 1) * 128] = total[:64]
            y_ref[block * 2 + 1, :, part * 128 : (part + 1) * 128] = total[64:]


def project(half, v, z):
    return pl.pallas_call(
        project_kernel,
        out_shape=jax.ShapeDtypeStruct((4, 64, 512), jnp.float32),
        in_specs=[IN_SMEM] + [IN_VMEM] * (1 + len(z)),
        out_specs=IN_VMEM,
        compiler_params=SMALL,
        cost_estimate=pl.CostEstimate(flops=3 * 512**3, bytes_accessed=2 * 2**20, transcendentals=0),
    )(half, v, *z)


def order_kernel(place_ref, *refs):
    for part, x_ref in enumerate(refs[:4]):
        refs[4][place_ref[0] ^ part] = x_ref[...]


def in_order(place, parts):
    return pl.pallas_call(
        order_kernel,
        out_shape=jax.ShapeDtypeStruct((4, *parts[0].shape), jnp.float32),
        in_specs=[IN_SMEM] + [IN_VMEM] * 4,
        out_specs=IN_VMEM,
        compiler_params=SMALL,
        cost_estimate=pl.CostEstimate(flops=2**20, bytes_accessed=2 * 2**20, transcendentals=0),
    )(place, *parts)


def exchange(x, axes):
    return lax.all_to_all(x, axes, 0, 0, tiled=True)


FLIP = [(0, 1), (1, 0)]


def body(moments, basis, slot_order):
    swap = lax.dynamic_slice_in_dim(slot_order, lax.axis_index("g"), 1)
    half = lax.axis_index("zl").astype(jnp.int32) ^ swap
    x_pos = lax.axis_index("xl")
    c_pos = lax.axis_index("c")
    row = lax.axis_index(ROW).astype(jnp.int32).reshape(1)
    basis_y = exchange(jnp.broadcast_to(basis, (4, 512, 128)), "y")
    by_x = lax.ppermute(moments, "xl", FLIP)
    by_c = lax.ppermute(moments, "c", FLIP)
    by_xc = lax.ppermute(by_x, "c", FLIP)

    turned = basis.T.reshape(2, 64, 512)
    got = []
    for step in range(2):
        routes = [(x * 2 + c, c * 2 + (x ^ step)) for x in range(2) for c in range(2)]
        piece = lax.dynamic_index_in_dim(turned, x_pos ^ step, 0, keepdims=False)
        got.append(lax.ppermute(piece, ("xl", "c"), routes))
    mixed = jnp.where(c_pos == 0, jnp.concatenate(got, 0), jnp.concatenate(got[::-1], 0))

    place = jnp.concatenate([swap, (x_pos * 2 + c_pos).astype(jnp.int32).reshape(1)])
    partial = image(place, (moments, by_c, by_x, by_xc), basis_y)
    summed = exchange(partial, ROW)

    parts = [mixed] + [lax.ppermute(mixed, ROW, [(p, p ^ m) for p in range(4)]) for m in (1, 2, 3)]
    basis_rows = exchange(in_order(row, parts), "y")

    total = (summed[0] + summed[1]) + (summed[2] + summed[3])
    z = [lax.all_gather(total[i * 256 : (i + 1) * 256], ("xl", "c"), axis=0) for i in range(2)]
    out = exchange(project(half, basis_rows, z), "y")
    return ((out[0] + out[1]) + (out[2] + out[3])).T


def solution(mesh):
    torus = Mesh(mesh.devices.reshape(mesh.shape["wide"] // 4, 2, 2, 4, 2, 2), ("g", *ROW, *COL))
    spec = P(("g", *ROW), COL)
    return jax.shard_map(body, mesh=torus, in_specs=(spec, spec, P()), out_specs=spec, check_vma=False)
```

time: 116 us -> 104 us (0.90)
  the two profiles are of different devices: /device:TPU:352 before, /device:TPU:4 now
where the time goes in v2:
time: 104 us; the launch traced here: 103 us
  starting transfers between devices  38.4 us (37%)
  blocking collectives  29.7 us (29%)
  waiting for transfers between devices  24.1 us (23%)
  Pallas kernels  5.42 us (5%)
  local copies, waits for them, and re-layouts  3.42 us (3%)
  other arithmetic  1.41 us (1%)
    all_to_all x3, starting transfers between devices, exchange(): return lax.all_to_all(x, axes, 0, 0, tiled=True)  15.6 us
    all_gather x2, blocking collectives, body(): lax.all_gather(total[i * 256:(i + 1) * 256], ('xl', 'c'), axis=0)  15.1 us
    all_to_all x1, blocking collectives, exchange(): return lax.all_to_all(x, axes, 0, 0, tiled=True)  14.6 us
    ppermute x3, starting transfers between devices, body(): lax.ppermute(mixed, ROW, [(p, p ^ m) for p in range(4)])  10.7 us
    ppermute x2, waiting for transfers between devices, body(): got.append(lax.ppermute(piece, ('xl', 'c'), routes))  9.85 us
    ppermute x3, waiting for transfers between devices, body(): lax.ppermute(mixed, ROW, [(p, p ^ m) for p in range(4)])  8.04 us
    ppermute x2, starting transfers between devices, body(): got.append(lax.ppermute(piece, ('xl', 'c'), routes))  5.13 us
    ppermute x1, waiting for transfers between devices, body(): by_x = lax.ppermute(moments, 'xl', FLIP)  4.62 us
  transfers between devices with their start and end apart: 11, of which 4 were waited for; matrix products, arithmetic and copies ran while one was open for 1% of the time, Pallas kernels for 1%

profile of v2, /device:TPU:4, one launch (start us, length us, event | category | flops | bytes accessed | tf_op | source)
XLA Modules:
  0.0 103.2 jit_solution(16706729848416835992)
XLA Ops:
  0.0 2.0 %broadcast_in_dim.3 = f32[4,512,128]{2,1,0:T(8,128)} broadcast(f32[512,128]{1,0:T(8,128)} %param.4), dimensions={1,2} | broadcast | bytes 1310720 | tf_op jit(solution)/shard_map/broadcast_in_dim | solution.py:112
  2.0 0.0 copy-start
  2.0 4.6 %all-to-all-start.1 = ((f32[4,512,128]{2,1,0:T(8,128)}), f32[4,512,128]{2,1,0:T(8,128)S(1)}, u32[]{:S(2)}, u32[]{:S(2)}) async-start(f32[4,512,128]{2,1,0:T(8,128)} %broadcast_in_dim.3), calls=%async_computation.1 | async-start | bytes 2097152 | tf_op jit(solution)/shard_map/all_to_all | solution.py:100
  6.6 0.0 copy-done
  6.6 3.1 %collective-permute-start.6 = (f32[512,128]{1,0:T(8,128)S(1)}, f32[512,128]{1,0:T(8,128)S(1)}, u32[]{:S(2)}, u32[]{:S(2)}) collective-permute-start(f32[512,128]{1,0:T(8,128)S(1)} %copy-done), channel_id=1, source_target_pairs={{0,2},{2,0},{1,3},{3,1},{4,6},{6,4},{5,7},{7,5},{8,10},{10,8},{9,1... | collective-permute-start | bytes 786440 | tf_op jit(solution)/shard_map/ppermute | solution.py:113
  9.7 1.9 %collective-permute-start.5 = (f32[512,128]{1,0:T(8,128)S(1)}, f32[512,128]{1,0:T(8,128)S(1)}, u32[]{:S(2)}, u32[]{:S(2)}) collective-permute-start(f32[512,128]{1,0:T(8,128)S(1)} %copy-done), channel_id=1, source_target_pairs={{0,1},{1,0},{2,3},{3,2},{4,5},{5,4},{6,7},{7,6},{8,9},{9,8},{10,11... | collective-permute-start | bytes 786440 | tf_op jit(solution)/shard_map/ppermute | solution.py:114
  11.6 4.6 %collective-permute-done.6.refs_2_ = f32[512,128]{1,0:T(8,128)S(1)} collective-permute-done((f32[512,128]{1,0:T(8,128)S(1)}, f32[512,128]{1,0:T(8,128)S(1)}, u32[]{:S(2)}, u32[]{:S(2)}) %collective-permute-start.6) | collective-permute-done | bytes 262176 | tf_op jit(solution)/shard_map/ppermute | solution.py:113
  16.2 1.9 %collective-permute-start.7 = (f32[512,128]{1,0:T(8,128)S(1)}, f32[512,128]{1,0:T(8,128)S(1)}, u32[]{:S(2)}, u32[]{:S(2)}) collective-permute-start(f32[512,128]{1,0:T(8,128)S(1)} %collective-permute-done.6.refs_2_), channel_id=1, source_target_pairs={{0,1},{1,0},{2,3},{3,2},{4,5},{5,4},{6,7},{7,6},{8,9},{9,8},{10,11... | collective-permute-start | bytes 786440 | tf_op jit(solution)/shard_map/ppermute | solution.py:115
  18.2 0.0 copy-start.2
  18.2 0.6 copy-done.2
  18.8 0.6 dynamic_slice.10
  19.4 0.6 pad_add_fusion.place_ref
  20.1 0.0 collective-permute-done.5.refs_1_
  20.1 0.0 collective-permute-done.7.refs_3_
  20.1 1.6 %all-to-all-done.1.refs_4_ = f32[4,512,128]{2,1,0:T(8,128)S(1)} async-done(((f32[4,512,128]{2,1,0:T(8,128)}), f32[4,512,128]{2,1,0:T(8,128)S(1)}, u32[]{:S(2)}, u32[]{:S(2)}) %all-to-all-start.1) | async-done | bytes 1048608 | tf_op jit(solution)/shard_map/all_to_all | solution.py:100
  21.7 3.4 %shard_map.38 = f32[4,512,128]{2,1,0:T(8,128)} custom-call(s32[2]{0:T(128)S(1)} %pad_add_fusion.place_ref, f32[512,128]{1,0:T(8,128)S(1)} %copy-done, f32[512,128]{1,0:T(8,128)S(1)} %collective-permute-done.5.refs_1_, f32[512,128]{1,0:T(8,128)S(1)} %collective-permute-done.6.refs_2_, f32[512,128]{1,0:T(8,128)S(1)} %collective-permute-done.7.refs_3_, ...), custom_call_target="tpu_custom_call" | custom-call | flops 805306368 | bytes 3145728 | tf_op jit(solution)/shard_map/pallas_call | solution.py:46
  25.1 0.0 copy-start.1
  25.1 6.3 %all-to-all-start.2 = ((f32[4,512,128]{2,1,0:T(8,128)}), f32[4,512,128]{2,1,0:T(8,128)S(1)}, u32[]{:S(2)}, u32[]{:S(2)}) async-start(f32[4,512,128]{2,1,0:T(8,128)} %shard_map.38), calls=%async_computation.2 | async-start | bytes 2097152 | tf_op jit(solution)/shard_map/all_to_all | solution.py:100
  31.4 0.0 copy-done.1
  31.4 0.1 copy.7
  31.5 0.7 collective-permute-start
  32.2 4.5 %collective-permute-start.1 = (f32[64,512]{1,0:T(8,128)S(1)}, f32[64,512]{1,0:T(8,128)S(1)}, u32[]{:S(2)}, u32[]{:S(2)}) collective-permute-start(f32[64,512]{1,0:T(8,128)S(1)} %get-tuple-element.8), channel_id=1, source_target_pairs={{0,1},{1,3},{2,0},{3,2},{4,5},{5,7},{6,4},{7,6},{8,9},{9,11},{10,8... | collective-permute-start | bytes 393224 | tf_op jit(solution)/shard_map/ppermute | solution.py:122
  36.7 0.0 collective-permute-done
  36.7 9.9 %collective-permute-done.1 = f32[64,512]{1,0:T(8,128)S(1)} collective-permute-done((f32[64,512]{1,0:T(8,128)S(1)}, f32[64,512]{1,0:T(8,128)S(1)}, u32[]{:S(2)}, u32[]{:S(2)}) %collective-permute-start.1) | collective-permute-done | bytes 131104 | tf_op jit(solution)/shard_map/ppermute | solution.py:122
  46.6 1.9 %collective-permute-start.2 = (f32[128,512]{1,0:T(8,128)S(1)}, f32[128,512]{1,0:T(8,128)S(1)}, u32[]{:S(2)}, u32[]{:S(2)}) collective-permute-start(f32[128,512]{1,0:T(8,128)S(1)} %maximum_select_fusion.refs_0_), channel_id=1, source_target_pairs={{0,16},{16,0},{32,48},{48,32},{1,17},{17,1},{33,49},{49,33},{2,18}... | collective-permute-start | bytes 786440 | tf_op jit(solution)/shard_map/ppermute | solution.py:129
  48.5 3.4 %collective-permute-start.3 = (f32[128,512]{1,0:T(8,128)S(1)}, f32[128,512]{1,0:T(8,128)S(1)}, u32[]{:S(2)}, u32[]{:S(2)}) collective-permute-start(f32[128,512]{1,0:T(8,128)S(1)} %maximum_select_fusion.refs_0_), channel_id=1, source_target_pairs={{0,32},{16,48},{32,0},{48,16},{1,33},{17,49},{33,1},{49,17},{2,34}... | collective-permute-start | bytes 786440 | tf_op jit(solution)/shard_map/ppermute | solution.py:129
  51.9 5.4 %collective-permute-start.4 = (f32[128,512]{1,0:T(8,128)S(1)}, f32[128,512]{1,0:T(8,128)S(1)}, u32[]{:S(2)}, u32[]{:S(2)}) collective-permute-start(f32[128,512]{1,0:T(8,128)S(1)} %maximum_select_fusion.refs_0_), channel_id=1, source_target_pairs={{0,48},{16,32},{32,16},{48,0},{1,49},{17,33},{33,17},{49,1},{2,50}... | collective-permute-start | bytes 786440 | tf_op jit(solution)/shard_map/ppermute | solution.py:129
  57.9 0.0 collective-permute-done.2.refs_1_
  57.9 0.0 collective-permute-done.3.refs_2_
  57.9 8.0 %collective-permute-done.4.refs_3_ = f32[128,512]{1,0:T(8,128)S(1)} collective-permute-done((f32[128,512]{1,0:T(8,128)S(1)}, f32[128,512]{1,0:T(8,128)S(1)}, u32[]{:S(2)}, u32[]{:S(2)}) %collective-permute-start.4) | collective-permute-done | bytes 262176 | tf_op jit(solution)/shard_map/ppermute | solution.py:129
  65.9 1.1 %shard_map.37 = f32[4,128,512]{2,1,0:T(8,128)} custom-call(s32[1]{0:T(128)} %bitcast.1.place_ref, f32[128,512]{1,0:T(8,128)S(1)} %maximum_select_fusion.refs_0_, f32[128,512]{1,0:T(8,128)S(1)} %collective-permute-done.2.refs_1_, f32[128,512]{1,0:T(8,128)S(1)} %collective-permute-done.3.refs_2_, f32[128,512]{1,0:T(8,128)S(1)} %collective-permute-done.4.refs_3_), custom_call_target="tpu_custom_call" | custom-call | flops 1048576 | bytes 2097152 | tf_op jit(solution)/shard_map/pallas_call | solution.py:89
  67.0 0.0 all-to-all-done.2
  67.0 4.7 %all-to-all-start = ((f32[4,128,512]{2,1,0:T(8,128)}), f32[4,128,512]{2,1,0:T(8,128)S(1)}, u32[]{:S(2)}, u32[]{:S(2)}) async-start(f32[4,128,512]{2,1,0:T(8,128)} %shard_map.37), calls=%async_computation | async-start | bytes 2097152 | tf_op jit(solution)/shard_map/all_to_all | solution.py:100
  71.8 0.1 fusion
  71.8 7.9 %all_gather.8.refs_0_ = f32[4,256,128]{2,1,0:T(8,128)S(1)} all-gather(f32[1,256,128]{2,1,0:T(8,128)S(1)} %get-tuple-element.6), channel_id=1, replica_groups=mesh['g'=8,'zl'=2,'xh'=2,'y'=4,'xl'=2,'c'=2] {'xl','c'}, dimensions={0}, use_global_device_ids=true | all-gather | bytes 655360 | tf_op jit(solution)/shard_map/all_gather | solution.py:133
  79.7 7.3 %all_gather.9.refs_1_ = f32[4,256,128]{2,1,0:T(8,128)S(1)} all-gather(f32[1,256,128]{2,1,0:T(8,128)S(1)} %get-tuple-element.5), channel_id=1, replica_groups=mesh['g'=8,'zl'=2,'xh'=2,'y'=4,'xl'=2,'c'=2] {'xl','c'}, dimensions={0}, use_global_device_ids=true | all-gather | bytes 655360 | tf_op jit(solution)/shard_map/all_gather | solution.py:133
  87.0 0.0 all-to-all-done.v_ref
  87.0 1.0 shard_map.39
  88.0 14.6 %all_to_all.20 = f32[4,64,512]{2,1,0:T(8,128)S(1)} all-to-all(f32[4,64,512]{2,1,0:T(8,128)S(1)} %shard_map.39), channel_id=1, replica_groups=mesh['g'=8,'zl'=2,'xh'=2,'y'=4,'xl'=2,'c'=2] {'y'}, dimensions={0} | all-to-all | bytes 1048576 | tf_op jit(solution)/shard_map/all_to_all | solution.py:100
  102.5 0.7 fusion.2
  (3 shorter events, 0.1 us)
Async XLA Ops:
  2.0 4.6 %copy-start = (f32[512,128]{1,0:T(8,128)S(1)}, f32[512,128]{1,0:T(8,128)}, u32[]{:S(2)}) copy-start(f32[512,128]{1,0:T(8,128)} %refs_0_.1) | copy-start | bytes 786436
  2.0 19.7 %all-to-all-start.1 = ((f32[4,512,128]{2,1,0:T(8,128)}), f32[4,512,128]{2,1,0:T(8,128)S(1)}, u32[]{:S(2)}, u32[]{:S(2)}) async-start(f32[4,512,128]{2,1,0:T(8,128)} %broadcast_in_dim.3), calls=%async_computation.1 | async-start | bytes 2097152 | tf_op jit(solution)/shard_map/all_to_all | solution.py:100
  6.6 9.6 %collective-permute-start.6 = (f32[512,128]{1,0:T(8,128)S(1)}, f32[512,128]{1,0:T(8,128)S(1)}, u32[]{:S(2)}, u32[]{:S(2)}) collective-permute-start(f32[512,128]{1,0:T(8,128)S(1)} %copy-done), channel_id=1, source_target_pairs={{0,2},{2,0},{1,3},{3,1},{4,6},{6,4},{5,7},{7,5},{8,10},{10,8},{9,1... | collective-permute-start | bytes 786440 | tf_op jit(solution)/shard_map/ppermute | solution.py:113
  9.7 10.4 %collective-permute-start.5 = (f32[512,128]{1,0:T(8,128)S(1)}, f32[512,128]{1,0:T(8,128)S(1)}, u32[]{:S(2)}, u32[]{:S(2)}) collective-permute-start(f32[512,128]{1,0:T(8,128)S(1)} %copy-done), channel_id=1, source_target_pairs={{0,1},{1,0},{2,3},{3,2},{4,5},{5,4},{6,7},{7,6},{8,9},{9,8},{10,11... | collective-permute-start | bytes 786440 | tf_op jit(solution)/shard_map/ppermute | solution.py:114
  16.2 3.8 %collective-permute-start.7 = (f32[512,128]{1,0:T(8,128)S(1)}, f32[512,128]{1,0:T(8,128)S(1)}, u32[]{:S(2)}, u32[]{:S(2)}) collective-permute-start(f32[512,128]{1,0:T(8,128)S(1)} %collective-permute-done.6.refs_2_), channel_id=1, source_target_pairs={{0,1},{1,0},{2,3},{3,2},{4,5},{5,4},{6,7},{7,6},{8,9},{9,8},{10,11... | collective-permute-start | bytes 786440 | tf_op jit(solution)/shard_map/ppermute | solution.py:115
  18.2 0.7 copy-start.2
  25.1 6.3 %copy-start.1 = (f32[512,128]{1,0:T(8,128)S(1)}, f32[512,128]{1,0:T(8,128)}, u32[]{:S(2)}) copy-start(f32[512,128]{1,0:T(8,128)} %param.4) | copy-start | bytes 786436
  25.1 41.9 %all-to-all-start.2 = ((f32[4,512,128]{2,1,0:T(8,128)}), f32[4,512,128]{2,1,0:T(8,128)S(1)}, u32[]{:S(2)}, u32[]{:S(2)}) async-start(f32[4,512,128]{2,1,0:T(8,128)} %shard_map.38), calls=%async_computation.2 | async-start | bytes 2097152 | tf_op jit(solution)/shard_map/all_to_all | solution.py:100
  31.5 5.2 %collective-permute-start = (f32[64,512]{1,0:T(8,128)S(1)}, f32[64,512]{1,0:T(8,128)S(1)}, u32[]{:S(2)}, u32[]{:S(2)}) collective-permute-start(f32[64,512]{1,0:T(8,128)S(1)} %get-tuple-element.7), channel_id=1, source_target_pairs={{0,0},{1,2},{2,1},{3,3},{4,4},{5,6},{6,5},{7,7},{8,8},{9,10},{10,9... | collective-permute-start | bytes 393224 | tf_op jit(solution)/shard_map/ppermute | solution.py:122
  32.2 14.3 %collective-permute-start.1 = (f32[64,512]{1,0:T(8,128)S(1)}, f32[64,512]{1,0:T(8,128)S(1)}, u32[]{:S(2)}, u32[]{:S(2)}) collective-permute-start(f32[64,512]{1,0:T(8,128)S(1)} %get-tuple-element.8), channel_id=1, source_target_pairs={{0,1},{1,3},{2,0},{3,2},{4,5},{5,7},{6,4},{7,6},{8,9},{9,11},{10,8... | collective-permute-start | bytes 393224 | tf_op jit(solution)/shard_map/ppermute | solution.py:122
  46.6 11.3 %collective-permute-start.2 = (f32[128,512]{1,0:T(8,128)S(1)}, f32[128,512]{1,0:T(8,128)S(1)}, u32[]{:S(2)}, u32[]{:S(2)}) collective-permute-start(f32[128,512]{1,0:T(8,128)S(1)} %maximum_select_fusion.refs_0_), channel_id=1, source_target_pairs={{0,16},{16,0},{32,48},{48,32},{1,17},{17,1},{33,49},{49,33},{2,18}... | collective-permute-start | bytes 786440 | tf_op jit(solution)/shard_map/ppermute | solution.py:129
  48.5 9.4 %collective-permute-start.3 = (f32[128,512]{1,0:T(8,128)S(1)}, f32[128,512]{1,0:T(8,128)S(1)}, u32[]{:S(2)}, u32[]{:S(2)}) collective-permute-start(f32[128,512]{1,0:T(8,128)S(1)} %maximum_select_fusion.refs_0_), channel_id=1, source_target_pairs={{0,32},{16,48},{32,0},{48,16},{1,33},{17,49},{33,1},{49,17},{2,34}... | collective-permute-start | bytes 786440 | tf_op jit(solution)/shard_map/ppermute | solution.py:129
  51.9 14.1 %collective-permute-start.4 = (f32[128,512]{1,0:T(8,128)S(1)}, f32[128,512]{1,0:T(8,128)S(1)}, u32[]{:S(2)}, u32[]{:S(2)}) collective-permute-start(f32[128,512]{1,0:T(8,128)S(1)} %maximum_select_fusion.refs_0_), channel_id=1, source_target_pairs={{0,48},{16,32},{32,16},{48,0},{1,49},{17,33},{33,17},{49,1},{2,50}... | collective-permute-start | bytes 786440 | tf_op jit(solution)/shard_map/ppermute | solution.py:129
  67.0 20.0 %all-to-all-start = ((f32[4,128,512]{2,1,0:T(8,128)}), f32[4,128,512]{2,1,0:T(8,128)S(1)}, u32[]{:S(2)}, u32[]{:S(2)}) async-start(f32[4,128,512]{2,1,0:T(8,128)} %shard_map.37), calls=%async_computation | async-start | bytes 2097152 | tf_op jit(solution)/shard_map/all_to_all | solution.py:100

commit v3 on v2

v3 whole, which is shorter than its diff:
```python
import functools

import jax
import jax.numpy as jnp
from jax import lax
from jax.experimental import pallas as pl
from jax.experimental.pallas import tpu as pltpu
from jax.sharding import Mesh
from jax.sharding import PartitionSpec as P


ROW = ("zl", "xh")
COL = ("y", "xl", "c")


def split(x):
    high = x.astype(jnp.bfloat16)
    return high, (x - high.astype(jnp.float32)).astype(jnp.bfloat16)


def product(left, right, dims):
    left_high, left_low = left
    right_high, right_low = right
    dot = functools.partial(lax.dot_general, dimension_numbers=(dims, ((), ())), preferred_element_type=jnp.float32)
    return dot(left_high, right_high) + (dot(left_high, right_low) + dot(left_low, right_high))


SMALL = pltpu.CompilerParams(vmem_limit_bytes=24 * 2**20)
IN_VMEM = pl.BlockSpec(memory_space=pltpu.VMEM)
IN_SMEM = pl.BlockSpec(memory_space=pltpu.SMEM)


def at(axis):
    return lax.axis_index(axis).astype(jnp.int32)


def image_kernel(swap, *refs):
    a_refs, v_ref, z_ref = refs[:4], refs[4], refs[5]
    column = at("xl") * 2 + at("c")
    rows = split(jnp.concatenate([a_ref[...] for a_ref in a_refs], axis=1))
    for slot in range(2):
        cols = split(jnp.concatenate([v_ref[(slot ^ swap) * 2], v_ref[(slot ^ swap) * 2 + 1]], axis=1))
        result = product(rows, cols, ((0,), (0,)))
        for part in range(4):
            start = pl.multiple_of((column ^ part) * 128, 128)
            for block in range(2):
                z_ref[slot * 2 + block, pl.ds(start, 128), :] = result[
                    part * 128 : (part + 1) * 128, block * 128 : (block + 1) * 128
                ]


def image(swap, a, v):
    return pl.pallas_call(
        functools.partial(image_kernel, swap),
        out_shape=jax.ShapeDtypeStruct((4, 512, 128), jnp.float32),
        in_specs=[IN_VMEM] * 5,
        out_specs=IN_VMEM,
        compiler_params=SMALL,
        cost_estimate=pl.CostEstimate(flops=6 * 512**3, bytes_accessed=3 * 2**20, transcendentals=0),
    )(*a, v)


def project_kernel(*refs):
    kept_refs, other_ref, mixed_ref, z_refs, y_ref = refs[:2], refs[2], refs[3], refs[4:8], refs[8]
    c_pos = at("c")
    column, block_pos = at("xl") * 2 + c_pos, at("y") % 2
    cols = split(jnp.concatenate([z_ref[...] for z_ref in z_refs], axis=1))
    own = pl.ds(pl.multiple_of(c_pos * 64, 64), 64)
    kept = jnp.where((at("xh") ^ block_pos) == 0, kept_refs[0][own, :], kept_refs[1][own, :])
    rows = split(jnp.concatenate([kept, mixed_ref[0], other_ref[own, :], mixed_ref[1]], axis=0))
    result = product(rows, cols, ((1,), (0,)))
    for block in range(2):
        for side in range(2):
            piece = (block_pos ^ block) * 2 + (c_pos ^ side)
            for part in range(4):
                start = pl.multiple_of((column ^ part) * 128, 128)
                first = (block * 2 + side) * 64
                y_ref[piece, :, pl.ds(start, 128)] = result[first : first + 64, part * 128 : (part + 1) * 128]


def project(kept, other, mixed, z):
    return pl.pallas_call(
        project_kernel,
        out_shape=jax.ShapeDtypeStruct((4, 64, 512), jnp.float32),
        in_specs=[IN_VMEM] * 8,
        out_specs=IN_VMEM,
        compiler_params=SMALL,
        cost_estimate=pl.CostEstimate(flops=3 * 512**3, bytes_accessed=2 * 2**20, transcendentals=0),
    )(*kept, other, mixed, *z)


def exchange(x, axes):
    return lax.all_to_all(x, axes, 0, 0, tiled=True)


def index(*bits):
    return functools.reduce(lambda total, bit: total * 2 + bit, bits, 0)


def turning(swap, step):
    routes = []
    for source in range(64):
        zl, xh, high, low, xl, c = (source >> shift & 1 for shift in range(5, -1, -1))
        routes.append((source, index(high ^ swap, xh ^ step, zl, low, c, xl)))
    return routes


FLIP = [(0, 1), (1, 0)]


def branch(swap, moments, basis):
    basis_y = exchange(jnp.broadcast_to(basis, (4, 512, 128)), "y")
    turned = basis.T
    by_x = lax.ppermute(moments, "xl", FLIP)
    by_c = lax.ppermute(moments, "c", FLIP)
    by_xc = lax.ppermute(by_x, "c", FLIP)
    kept = [lax.ppermute(turned, (*ROW, *COL), turning(swap, m)) for m in range(2)]
    partial = image(swap, (moments, by_c, by_x, by_xc), basis_y)
    summed = exchange(partial, ROW)

    low = at("y") % 2
    keep_first = (at("xh") ^ low) == 0
    away = jnp.where(keep_first, kept[1], kept[0])
    other = lax.ppermute(away, "y", [(y, y ^ 1) for y in range(4)])
    c_pos = lax.axis_index("c")
    cross = jnp.stack([jnp.where(keep_first, kept[0], kept[1]), other]).reshape(2, 2, 64, 512)
    mixed = lax.ppermute(lax.dynamic_index_in_dim(cross, 1 - c_pos, 1, keepdims=False), "c", FLIP)

    total = (summed[0] + summed[1]) + (summed[2] + summed[3])
    z_x = lax.ppermute(total, "xl", FLIP)
    z_c = lax.ppermute(total, "c", FLIP)
    z_xc = lax.ppermute(z_x, "c", FLIP)
    out = exchange(project(kept, other, mixed, (total, z_c, z_x, z_xc)), "y")
    return ((out[0] + out[1]) + (out[2] + out[3])).T


def body(moments, basis, slot_order):
    swap = lax.dynamic_index_in_dim(slot_order, lax.axis_index("g"), 0, keepdims=False)
    return lax.cond(swap == 0, functools.partial(branch, 0), functools.partial(branch, 1), moments, basis)


def solution(mesh):
    torus = Mesh(mesh.devices.reshape(mesh.shape["wide"] // 4, 2, 2, 4, 2, 2), ("g", *ROW, *COL))
    spec = P(("g", *ROW), COL)
    return jax.shard_map(body, mesh=torus, in_specs=(spec, spec, P()), out_specs=spec, check_vma=False)
```

time: 104 us -> 93.6 us (0.90)
  the two profiles are of different devices: /device:TPU:4 before, /device:TPU:192 now
where the time goes in v3:
time: 93.6 us; the launch traced here: 93 us
  starting transfers between devices  35.1 us (38%)
  waiting for transfers between devices  32.4 us (35%)
  blocking collectives  17.8 us (19%)
  local copies, waits for them, and re-layouts  4.01 us (4%)
  Pallas kernels  2.62 us (3%)
    ppermute x2, waiting for transfers between devices, branch(): lax.ppermute(turned, (*ROW, *COL), turning(swap, m))  19 us
    all_to_all x1, blocking collectives, exchange(): return lax.all_to_all(x, axes, 0, 0, tiled=True)  17.8 us
    all_to_all x2, starting transfers between devices, exchange(): return lax.all_to_all(x, axes, 0, 0, tiled=True)  10.4 us
    ppermute x2, starting transfers between devices, branch(): lax.ppermute(turned, (*ROW, *COL), turning(swap, m))  6.11 us
    ppermute x1, waiting for transfers between devices, branch(): by_x = lax.ppermute(moments, 'xl', FLIP)  4.32 us
    ppermute x1, waiting for transfers between devices, branch(): other = lax.ppermute(away, 'y', [(y, y ^ 1) for y in range(4)])  4.12 us
    ppermute x1, starting transfers between devices, branch(): by_x = lax.ppermute(moments, 'xl', FLIP)  3.39 us
    ppermute x1, starting transfers between devices, branch(): other = lax.ppermute(away, 'y', [(y, y ^ 1) for y in range(4)])  3.07 us
  transfers between devices with their start and end apart: 12, of which 6 were waited for; matrix products, arithmetic and copies ran while one was open for 0% of the time, Pallas kernels for 0%

profile of v3, /device:TPU:192, one launch (start us, length us, event | category | flops | bytes accessed | tf_op | source)
XLA Modules:
  0.0 93.0 jit_solution(1057884314207405134)
XLA Ops:
  0.0 0.0 copy-start.5
  0.0 0.7 copy-done.5
  0.7 0.6 dynamic_slice.11
  1.9 90.4 %conditional.1 = (f32[512,64]{0,1:T(8,128)S(1)}) conditional(s32[]{:T(128)} %bitcast.24, (f32[512,128]{1,0:T(8,128)}, f32[512,128]{1,0:T(8,128)}) %tuple.11, (f32[512,128]{1,0:T(8,128)}, f32[512,128]{1,0:T(8,128)}) %tuple.11), branch_computations={%region_0.1_spmd, %region_1.2_spmd} | conditional | flops 1208451072 | bytes 30802712 | solution.py:139
  1.9 2.0 %broadcast_in_dim.5 = f32[4,512,128]{2,1,0:T(8,128)} broadcast(f32[512,128]{1,0:T(8,128)} %get-tuple-element.23), dimensions={1,2} | broadcast | bytes 1310720 | tf_op jit(solution)/shard_map/cond/branch_1_fun/broadcast_in_dim | solution.py:112
  3.9 0.0 copy-start.3
  3.9 4.6 %all-to-all-start.3 = ((f32[4,512,128]{2,1,0:T(8,128)}), f32[4,512,128]{2,1,0:T(8,128)S(1)}, u32[]{:S(2)}, u32[]{:S(2)}) async-start(f32[4,512,128]{2,1,0:T(8,128)} %broadcast_in_dim.5), calls=%async_computation.3 | async-start | bytes 2097152 | tf_op jit(solution)/shard_map/cond/branch_1_fun/all_to_all | solution.py:93
  8.5 0.0 copy-done.3
  8.5 3.4 %collective-permute-start.15 = (f32[512,128]{1,0:T(8,128)S(1)}, f32[512,128]{1,0:T(8,128)S(1)}, u32[]{:S(2)}, u32[]{:S(2)}) collective-permute-start(f32[512,128]{1,0:T(8,128)S(1)} %copy-done.3), channel_id=1, source_target_pairs={{0,2},{2,0},{1,3},{3,1},{4,6},{6,4},{5,7},{7,5},{8,10},{10,8},{9,1... | collective-permute-start | bytes 786440 | tf_op jit(solution)/shard_map/cond/branch_1_fun/ppermute | solution.py:114
  11.9 1.9 %collective-permute-start.14 = (f32[512,128]{1,0:T(8,128)S(1)}, f32[512,128]{1,0:T(8,128)S(1)}, u32[]{:S(2)}, u32[]{:S(2)}) collective-permute-start(f32[512,128]{1,0:T(8,128)S(1)} %copy-done.3), channel_id=1, source_target_pairs={{0,1},{1,0},{2,3},{3,2},{4,5},{5,4},{6,7},{7,6},{8,9},{9,8},{10,11... | collective-permute-start | bytes 786440 | tf_op jit(solution)/shard_map/cond/branch_1_fun/ppermute | solution.py:115
  13.8 4.3 %collective-permute-done.15.refs_2_ = f32[512,128]{1,0:T(8,128)S(1)} collective-permute-done((f32[512,128]{1,0:T(8,128)S(1)}, f32[512,128]{1,0:T(8,128)S(1)}, u32[]{:S(2)}, u32[]{:S(2)}) %collective-permute-start.15) | collective-permute-done | bytes 262176 | tf_op jit(solution)/shard_map/cond/branch_1_fun/ppermute | solution.py:114
  18.2 1.9 %collective-permute-start.16 = (f32[512,128]{1,0:T(8,128)S(1)}, f32[512,128]{1,0:T(8,128)S(1)}, u32[]{:S(2)}, u32[]{:S(2)}) collective-permute-start(f32[512,128]{1,0:T(8,128)S(1)} %collective-permute-done.15.refs_2_), channel_id=1, source_target_pairs={{0,1},{1,0},{2,3},{3,2},{4,5},{5,4},{6,7},{7,6},{8,9},{9,8},{10,11... | collective-permute-start | bytes 786440 | tf_op jit(solution)/shard_map/cond/branch_1_fun/ppermute | solution.py:116
  20.1 0.0 collective-permute-done.14.refs_1_
  20.1 1.5 %collective-permute-done.16.refs_3_ = f32[512,128]{1,0:T(8,128)S(1)} collective-permute-done((f32[512,128]{1,0:T(8,128)S(1)}, f32[512,128]{1,0:T(8,128)S(1)}, u32[]{:S(2)}, u32[]{:S(2)}) %collective-permute-start.16) | collective-permute-done | bytes 262176 | tf_op jit(solution)/shard_map/cond/branch_1_fun/ppermute | solution.py:116
  21.6 2.0 %all-to-all-done.3.refs_4_ = f32[4,512,128]{2,1,0:T(8,128)S(1)} async-done(((f32[4,512,128]{2,1,0:T(8,128)}), f32[4,512,128]{2,1,0:T(8,128)S(1)}, u32[]{:S(2)}, u32[]{:S(2)}) %all-to-all-start.3) | async-done | bytes 1048608 | tf_op jit(solution)/shard_map/cond/branch_1_fun/all_to_all | solution.py:93
  23.6 2.0 %branch_1_fun.2 = f32[4,512,128]{2,1,0:T(8,128)} custom-call(f32[512,128]{1,0:T(8,128)S(1)} %copy-done.3, f32[512,128]{1,0:T(8,128)S(1)} %collective-permute-done.14.refs_1_, f32[512,128]{1,0:T(8,128)S(1)} %collective-permute-done.15.refs_2_, f32[512,128]{1,0:T(8,128)S(1)} %collective-permute-done.16.refs_3_, f32[4,512,128]{2,1,0:T(8,128)S(1)} %all-to-all-done.3.refs_4_), custom_call_target="tpu_custom_call" | custom-call | flops 805306368 | bytes 3145728 | tf_op jit(solution)/shard_map/cond/branch_1_fun/pallas_call | solution.py:53
  25.6 0.0 copy-start.1
  25.6 5.8 %all-to-all-start.4 = ((f32[4,512,128]{2,1,0:T(8,128)}), f32[4,512,128]{2,1,0:T(8,128)S(1)}, u32[]{:S(2)}, u32[]{:S(2)}) async-start(f32[4,512,128]{2,1,0:T(8,128)} %branch_1_fun.2), calls=%async_computation.4 | async-start | bytes 2097152 | tf_op jit(solution)/shard_map/cond/branch_1_fun/all_to_all | solution.py:93
  31.4 0.0 copy-done.1
  31.4 0.1 copy.13
  31.5 5.4 %collective-permute-start.11 = (f32[128,512]{1,0:T(8,128)S(1)}, f32[128,512]{1,0:T(8,128)S(1)}, u32[]{:S(2)}, u32[]{:S(2)}) collective-permute-start(f32[128,512]{1,0:T(8,128)S(1)} %bitcast.37), channel_id=1, source_target_pairs={{0,16},{1,18},{2,17},{3,19},{4,20},{5,22},{6,21},{7,23},{8,48},{9,... | collective-permute-start | bytes 786440 | tf_op jit(solution)/shard_map/cond/branch_1_fun/ppermute | solution.py:117
  37.0 0.7 collective-permute-start.10
  37.7 19.0 %collective-permute-done.11.refs_1_ = f32[128,512]{1,0:T(8,128)S(1)} collective-permute-done((f32[128,512]{1,0:T(8,128)S(1)}, f32[128,512]{1,0:T(8,128)S(1)}, u32[]{:S(2)}, u32[]{:S(2)}) %collective-permute-start.11) | collective-permute-done | bytes 262176 | tf_op jit(solution)/shard_map/cond/branch_1_fun/ppermute | solution.py:117
  56.6 0.0 collective-permute-done.10.refs_0_
  56.7 3.1 %collective-permute-start.12 = (f32[128,512]{1,0:T(8,128)S(1)}, f32[128,512]{1,0:T(8,128)S(1)}, u32[]{:S(2)}, u32[]{:S(2)}) collective-permute-start(f32[128,512]{1,0:T(8,128)S(1)} %get-tuple-element.28), channel_id=1, source_target_pairs={{0,4},{4,0},{8,12},{12,8},{1,5},{5,1},{9,13},{13,9},{2,6},{6,2},{1... | collective-permute-start | bytes 786440 | tf_op jit(solution)/shard_map/cond/branch_1_fun/ppermute | solution.py:124
  59.8 0.0 all-to-all-done.4
  59.8 0.1 fusion.9.refs_4_
  59.8 2.1 %collective-permute-start.18 = (f32[512,128]{1,0:T(8,128)S(1)}, f32[512,128]{1,0:T(8,128)S(1)}, u32[]{:S(2)}, u32[]{:S(2)}) collective-permute-start(f32[512,128]{1,0:T(8,128)S(1)} %fusion.9.refs_4_), channel_id=1, source_target_pairs={{0,2},{2,0},{1,3},{3,1},{4,6},{6,4},{5,7},{7,5},{8,10},{10,8},{9,1... | collective-permute-start | bytes 786440 | tf_op jit(solution)/shard_map/cond/branch_1_fun/ppermute | solution.py:130
  61.9 4.1 %collective-permute-done.12.refs_2_ = f32[128,512]{1,0:T(8,128)S(1)} collective-permute-done((f32[128,512]{1,0:T(8,128)S(1)}, f32[128,512]{1,0:T(8,128)S(1)}, u32[]{:S(2)}, u32[]{:S(2)}) %collective-permute-start.12) | collective-permute-done | bytes 262176 | tf_op jit(solution)/shard_map/cond/branch_1_fun/ppermute | solution.py:124
  66.1 1.9 %collective-permute-start.13 = (f32[2,64,512]{2,1,0:T(8,128)S(1)}, f32[2,64,512]{2,1,0:T(8,128)S(1)}, u32[]{:S(2)}, u32[]{:S(2)}) collective-permute-start(f32[2,64,512]{2,1,0:T(8,128)S(1)} %fusion.7), channel_id=1, source_target_pairs={{0,1},{1,0},{2,3},{3,2},{4,5},{5,4},{6,7},{7,6},{8,9},{9,8},{10,11... | collective-permute-start | bytes 786440 | tf_op jit(solution)/shard_map/cond/branch_1_fun/ppermute | solution.py:127
  68.0 2.4 %collective-permute-start.17 = (f32[512,128]{1,0:T(8,128)S(1)}, f32[512,128]{1,0:T(8,128)S(1)}, u32[]{:S(2)}, u32[]{:S(2)}) collective-permute-start(f32[512,128]{1,0:T(8,128)S(1)} %fusion.9.refs_4_), channel_id=1, source_target_pairs={{0,1},{1,0},{2,3},{3,2},{4,5},{5,4},{6,7},{7,6},{8,9},{9,8},{10,11... | collective-permute-start | bytes 786440 | tf_op jit(solution)/shard_map/cond/branch_1_fun/ppermute | solution.py:131
  70.4 0.0 collective-permute-done.18.refs_6_
  70.4 1.9 %collective-permute-start.19 = (f32[512,128]{1,0:T(8,128)S(1)}, f32[512,128]{1,0:T(8,128)S(1)}, u32[]{:S(2)}, u32[]{:S(2)}) collective-permute-start(f32[512,128]{1,0:T(8,128)S(1)} %collective-permute-done.18.refs_6_), channel_id=1, source_target_pairs={{0,1},{1,0},{2,3},{3,2},{4,5},{5,4},{6,7},{7,6},{8,9},{9,8},{10,11... | collective-permute-start | bytes 786440 | tf_op jit(solution)/shard_map/cond/branch_1_fun/ppermute | solution.py:132
  72.4 0.0 collective-permute-done.13.refs_3_
  72.4 0.0 collective-permute-done.17.refs_5_
  72.4 1.5 %collective-permute-done.19.refs_7_ = f32[512,128]{1,0:T(8,128)S(1)} collective-permute-done((f32[512,128]{1,0:T(8,128)S(1)}, f32[512,128]{1,0:T(8,128)S(1)}, u32[]{:S(2)}, u32[]{:S(2)}) %collective-permute-start.19) | collective-permute-done | bytes 262176 | tf_op jit(solution)/shard_map/cond/branch_1_fun/ppermute | solution.py:132
  73.9 0.6 branch_1_fun.3
  74.5 17.8 %all_to_all.25 = f32[4,64,512]{2,1,0:T(8,128)S(1)} all-to-all(f32[4,64,512]{2,1,0:T(8,128)S(1)} %branch_1_fun.3), channel_id=1, replica_groups=mesh['g'=8,'zl'=2,'xh'=2,'y'=4,'xl'=2,'c'=2] {'y'}, dimensions={0} | all-to-all | bytes 1048576 | tf_op jit(solution)/shard_map/cond/branch_1_fun/all_to_all | solution.py:93
  92.3 0.0 copy-start.4
  92.3 0.6 copy-done.4
  (3 shorter events, 0.1 us)
Async XLA Ops:
  0.0 0.7 copy-start.5
  3.9 4.6 %copy-start.3 = (f32[512,128]{1,0:T(8,128)S(1)}, f32[512,128]{1,0:T(8,128)}, u32[]{:S(2)}) copy-start(f32[512,128]{1,0:T(8,128)} %get-tuple-element.19.refs_0_) | copy-start | bytes 786436 | tf_op jit(solution)/shard_map/cond
  3.9 19.7 %all-to-all-start.3 = ((f32[4,512,128]{2,1,0:T(8,128)}), f32[4,512,128]{2,1,0:T(8,128)S(1)}, u32[]{:S(2)}, u32[]{:S(2)}) async-start(f32[4,512,128]{2,1,0:T(8,128)} %broadcast_in_dim.5), calls=%async_computation.3 | async-start | bytes 2097152 | tf_op jit(solution)/shard_map/cond/branch_1_fun/all_to_all | solution.py:93
  8.5 9.6 %collective-permute-start.15 = (f32[512,128]{1,0:T(8,128)S(1)}, f32[512,128]{1,0:T(8,128)S(1)}, u32[]{:S(2)}, u32[]{:S(2)}) collective-permute-start(f32[512,128]{1,0:T(8,128)S(1)} %copy-done.3), channel_id=1, source_target_pairs={{0,2},{2,0},{1,3},{3,1},{4,6},{6,4},{5,7},{7,5},{8,10},{10,8},{9,1... | collective-permute-start | bytes 786440 | tf_op jit(solution)/shard_map/cond/branch_1_fun/ppermute | solution.py:114
  11.9 8.2 %collective-permute-start.14 = (f32[512,128]{1,0:T(8,128)S(1)}, f32[512,128]{1,0:T(8,128)S(1)}, u32[]{:S(2)}, u32[]{:S(2)}) collective-permute-start(f32[512,128]{1,0:T(8,128)S(1)} %copy-done.3), channel_id=1, source_target_pairs={{0,1},{1,0},{2,3},{3,2},{4,5},{5,4},{6,7},{7,6},{8,9},{9,8},{10,11... | collective-permute-start | bytes 786440 | tf_op jit(solution)/shard_map/cond/branch_1_fun/ppermute | solution.py:115
  18.2 3.4 %collective-permute-start.16 = (f32[512,128]{1,0:T(8,128)S(1)}, f32[512,128]{1,0:T(8,128)S(1)}, u32[]{:S(2)}, u32[]{:S(2)}) collective-permute-start(f32[512,128]{1,0:T(8,128)S(1)} %collective-permute-done.15.refs_2_), channel_id=1, source_target_pairs={{0,1},{1,0},{2,3},{3,2},{4,5},{5,4},{6,7},{7,6},{8,9},{9,8},{10,11... | collective-permute-start | bytes 786440 | tf_op jit(solution)/shard_map/cond/branch_1_fun/ppermute | solution.py:116
  25.6 5.8 %copy-start.1 = (f32[512,128]{1,0:T(8,128)S(1)}, f32[512,128]{1,0:T(8,128)}, u32[]{:S(2)}) copy-start(f32[512,128]{1,0:T(8,128)} %get-tuple-element.23) | copy-start | bytes 786436 | tf_op jit(solution)/shard_map/cond
  25.6 34.2 %all-to-all-start.4 = ((f32[4,512,128]{2,1,0:T(8,128)}), f32[4,512,128]{2,1,0:T(8,128)S(1)}, u32[]{:S(2)}, u32[]{:S(2)}) async-start(f32[4,512,128]{2,1,0:T(8,128)} %branch_1_fun.2), calls=%async_computation.4 | async-start | bytes 2097152 | tf_op jit(solution)/shard_map/cond/branch_1_fun/all_to_all | solution.py:93
  31.5 25.1 %collective-permute-start.11 = (f32[128,512]{1,0:T(8,128)S(1)}, f32[128,512]{1,0:T(8,128)S(1)}, u32[]{:S(2)}, u32[]{:S(2)}) collective-permute-start(f32[128,512]{1,0:T(8,128)S(1)} %bitcast.37), channel_id=1, source_target_pairs={{0,16},{1,18},{2,17},{3,19},{4,20},{5,22},{6,21},{7,23},{8,48},{9,... | collective-permute-start | bytes 786440 | tf_op jit(solution)/shard_map/cond/branch_1_fun/ppermute | solution.py:117
  37.0 19.7 %collective-permute-start.10 = (f32[128,512]{1,0:T(8,128)S(1)}, f32[128,512]{1,0:T(8,128)S(1)}, u32[]{:S(2)}, u32[]{:S(2)}) collective-permute-start(f32[128,512]{1,0:T(8,128)S(1)} %bitcast.38), channel_id=1, source_target_pairs={{0,0},{1,2},{2,1},{3,3},{4,4},{5,6},{6,5},{7,7},{8,32},{9,34},{10,... | collective-permute-start | bytes 786440 | tf_op jit(solution)/shard_map/cond/branch_1_fun/ppermute | solution.py:117
  56.7 9.4 %collective-permute-start.12 = (f32[128,512]{1,0:T(8,128)S(1)}, f32[128,512]{1,0:T(8,128)S(1)}, u32[]{:S(2)}, u32[]{:S(2)}) collective-permute-start(f32[128,512]{1,0:T(8,128)S(1)} %get-tuple-element.28), channel_id=1, source_target_pairs={{0,4},{4,0},{8,12},{12,8},{1,5},{5,1},{9,13},{13,9},{2,6},{6,2},{1... | collective-permute-start | bytes 786440 | tf_op jit(solution)/shard_map/cond/branch_1_fun/ppermute | solution.py:124
  59.8 10.6 %collective-permute-start.18 = (f32[512,128]{1,0:T(8,128)S(1)}, f32[512,128]{1,0:T(8,128)S(1)}, u32[]{:S(2)}, u32[]{:S(2)}) collective-permute-start(f32[512,128]{1,0:T(8,128)S(1)} %fusion.9.refs_4_), channel_id=1, source_target_pairs={{0,2},{2,0},{1,3},{3,1},{4,6},{6,4},{5,7},{7,5},{8,10},{10,8},{9,1... | collective-permute-start | bytes 786440 | tf_op jit(solution)/shard_map/cond/branch_1_fun/ppermute | solution.py:130
  66.1 6.3 %collective-permute-start.13 = (f32[2,64,512]{2,1,0:T(8,128)S(1)}, f32[2,64,512]{2,1,0:T(8,128)S(1)}, u32[]{:S(2)}, u32[]{:S(2)}) collective-permute-start(f32[2,64,512]{2,1,0:T(8,128)S(1)} %fusion.7), channel_id=1, source_target_pairs={{0,1},{1,0},{2,3},{3,2},{4,5},{5,4},{6,7},{7,6},{8,9},{9,8},{10,11... | collective-permute-start | bytes 786440 | tf_op jit(solution)/shard_map/cond/branch_1_fun/ppermute | solution.py:127
  68.0 4.4 %collective-permute-start.17 = (f32[512,128]{1,0:T(8,128)S(1)}, f32[512,128]{1,0:T(8,128)S(1)}, u32[]{:S(2)}, u32[]{:S(2)}) collective-permute-start(f32[512,128]{1,0:T(8,128)S(1)} %fusion.9.refs_4_), channel_id=1, source_target_pairs={{0,1},{1,0},{2,3},{3,2},{4,5},{5,4},{6,7},{7,6},{8,9},{9,8},{10,11... | collective-permute-start | bytes 786440 | tf_op jit(solution)/shard_map/cond/branch_1_fun/ppermute | solution.py:131
  70.4 3.4 %collective-permute-start.19 = (f32[512,128]{1,0:T(8,128)S(1)}, f32[512,128]{1,0:T(8,128)S(1)}, u32[]{:S(2)}, u32[]{:S(2)}) collective-permute-start(f32[512,128]{1,0:T(8,128)S(1)} %collective-permute-done.18.refs_6_), channel_id=1, source_target_pairs={{0,1},{1,0},{2,3},{3,2},{4,5},{5,4},{6,7},{7,6},{8,9},{9,8},{10,11... | collective-permute-start | bytes 786440 | tf_op jit(solution)/shard_map/cond/branch_1_fun/ppermute | solution.py:132
  92.3 0.7 copy-start.4

commit v4 on v3

--- a/solution.py
+++ b/solution.py
@@ -60,10 +60,11 @@
     )(*a, v)
 
 
-def project_kernel(*refs):
+def project_kernel(swap, *refs):
     kept_refs, other_ref, mixed_ref, z_refs, y_ref = refs[:2], refs[2], refs[3], refs[4:8], refs[8]
     c_pos = at("c")
     column, block_pos = at("xl") * 2 + c_pos, at("y") % 2
+    first_block = block_pos ^ (at("y") // 2) ^ at("zl") ^ swap
     cols = split(jnp.concatenate([z_ref[...] for z_ref in z_refs], axis=1))
     own = pl.ds(pl.multiple_of(c_pos * 64, 64), 64)
     kept = jnp.where((at("xh") ^ block_pos) == 0, kept_refs[0][own, :], kept_refs[1][own, :])
@@ -71,16 +72,16 @@
     result = product(rows, cols, ((1,), (0,)))
     for block in range(2):
         for side in range(2):
-            piece = (block_pos ^ block) * 2 + (c_pos ^ side)
+            piece = (first_block ^ block) * 2 + (c_pos ^ side)
             for part in range(4):
                 start = pl.multiple_of((column ^ part) * 128, 128)
                 first = (block * 2 + side) * 64
                 y_ref[piece, :, pl.ds(start, 128)] = result[first : first + 64, part * 128 : (part + 1) * 128]
 
 
-def project(kept, other, mixed, z):
+def project(swap, kept, other, mixed, z):
     return pl.pallas_call(
-        project_kernel,
+        functools.partial(project_kernel, swap),
         out_shape=jax.ShapeDtypeStruct((4, 64, 512), jnp.float32),
         in_specs=[IN_VMEM] * 8,
         out_specs=IN_VMEM,
@@ -101,7 +102,7 @@
     routes = []
     for source in range(64):
         zl, xh, high, low, xl, c = (source >> shift & 1 for shift in range(5, -1, -1))
-        routes.append((source, index(high ^ swap, xh ^ step, zl, low, c, xl)))
+        routes.append((source, index(high ^ swap, xh ^ step, zl, low ^ zl ^ high, c, xl)))
     return routes
 
 
@@ -130,7 +131,7 @@
     z_x = lax.ppermute(total, "xl", FLIP)
     z_c = lax.ppermute(total, "c", FLIP)
     z_xc = lax.ppermute(z_x, "c", FLIP)
-    out = exchange(project(kept, other, mixed, (total, z_c, z_x, z_xc)), "y")
+    out = exchange(project(swap, kept, other, mixed, (total, z_c, z_x, z_xc)), "y")
     return ((out[0] + out[1]) + (out[2] + out[3])).T
 
 

time: 93.6 us -> 93 us (level)
  no operation moved by 1% of the time
where the time goes in v4:
time: 93 us; the launch traced here: 92.4 us
  starting transfers between devices  35.1 us (38%)
  waiting for transfers between devices  32.2 us (35%)
  blocking collectives  17.5 us (19%)
  local copies, waits for them, and re-layouts  4.01 us (4%)
  Pallas kernels  2.62 us (3%)
    ppermute x2, waiting for transfers between devices, branch(): lax.ppermute(turned, (*ROW, *COL), turning(swap, m))  19 us
    all_to_all x1, blocking collectives, exchange(): return lax.all_to_all(x, axes, 0, 0, tiled=True)  17.5 us
    all_to_all x2, starting transfers between devices, exchange(): return lax.all_to_all(x, axes, 0, 0, tiled=True)  10.4 us
    ppermute x2, starting transfers between devices, branch(): lax.ppermute(turned, (*ROW, *COL), turning(swap, m))  6.11 us
    ppermute x1, waiting for transfers between devices, branch(): by_x = lax.ppermute(moments, 'xl', FLIP)  4.32 us
    ppermute x1, waiting for transfers between devices, branch(): other = lax.ppermute(away, 'y', [(y, y ^ 1) for y in range(4)])  3.9 us
    ppermute x1, starting transfers between devices, branch(): by_x = lax.ppermute(moments, 'xl', FLIP)  3.39 us
    ppermute x1, starting transfers between devices, branch(): other = lax.ppermute(away, 'y', [(y, y ^ 1) for y in range(4)])  3.07 us
  transfers between devices with their start and end apart: 12, of which 6 were waited for; matrix products, arithmetic and copies ran while one was open for 0% of the time, Pallas kernels for 0%

profile of v4, /device:TPU:192, one launch (start us, length us, event | category | flops | bytes accessed | tf_op | source)
XLA Modules:
  0.0 92.4 jit_solution(13923093127790638481)
XLA Ops:
  0.0 0.0 copy-start.5
  0.0 0.7 copy-done.5
  0.7 0.6 dynamic_slice.11
  1.9 89.8 %conditional.1 = (f32[512,64]{0,1:T(8,128)S(1)}) conditional(s32[]{:T(128)} %bitcast.24, (f32[512,128]{1,0:T(8,128)}, f32[512,128]{1,0:T(8,128)}) %tuple.11, (f32[512,128]{1,0:T(8,128)}, f32[512,128]{1,0:T(8,128)}) %tuple.11), branch_computations={%region_0.1_spmd, %region_1.2_spmd} | conditional | flops 1208451072 | bytes 30802712 | solution.py:140
  1.9 2.0 %broadcast_in_dim.5 = f32[4,512,128]{2,1,0:T(8,128)} broadcast(f32[512,128]{1,0:T(8,128)} %get-tuple-element.23), dimensions={1,2} | broadcast | bytes 1310720 | tf_op jit(solution)/shard_map/cond/branch_1_fun/broadcast_in_dim | solution.py:113
  3.9 0.0 copy-start.3
  3.9 4.6 %all-to-all-start.3 = ((f32[4,512,128]{2,1,0:T(8,128)}), f32[4,512,128]{2,1,0:T(8,128)S(1)}, u32[]{:S(2)}, u32[]{:S(2)}) async-start(f32[4,512,128]{2,1,0:T(8,128)} %broadcast_in_dim.5), calls=%async_computation.3 | async-start | bytes 2097152 | tf_op jit(solution)/shard_map/cond/branch_1_fun/all_to_all | solution.py:94
  8.5 0.0 copy-done.3
  8.5 3.4 %collective-permute-start.15 = (f32[512,128]{1,0:T(8,128)S(1)}, f32[512,128]{1,0:T(8,128)S(1)}, u32[]{:S(2)}, u32[]{:S(2)}) collective-permute-start(f32[512,128]{1,0:T(8,128)S(1)} %copy-done.3), channel_id=1, source_target_pairs={{0,2},{2,0},{1,3},{3,1},{4,6},{6,4},{5,7},{7,5},{8,10},{10,8},{9,1... | collective-permute-start | bytes 786440 | tf_op jit(solution)/shard_map/cond/branch_1_fun/ppermute | solution.py:115
  11.9 1.9 %collective-permute-start.14 = (f32[512,128]{1,0:T(8,128)S(1)}, f32[512,128]{1,0:T(8,128)S(1)}, u32[]{:S(2)}, u32[]{:S(2)}) collective-permute-start(f32[512,128]{1,0:T(8,128)S(1)} %copy-done.3), channel_id=1, source_target_pairs={{0,1},{1,0},{2,3},{3,2},{4,5},{5,4},{6,7},{7,6},{8,9},{9,8},{10,11... | collective-permute-start | bytes 786440 | tf_op jit(solution)/shard_map/cond/branch_1_fun/ppermute | solution.py:116
  13.8 4.3 %collective-permute-done.15.refs_2_ = f32[512,128]{1,0:T(8,128)S(1)} collective-permute-done((f32[512,128]{1,0:T(8,128)S(1)}, f32[512,128]{1,0:T(8,128)S(1)}, u32[]{:S(2)}, u32[]{:S(2)}) %collective-permute-start.15) | collective-permute-done | bytes 262176 | tf_op jit(solution)/shard_map/cond/branch_1_fun/ppermute | solution.py:115
  18.2 1.9 %collective-permute-start.16 = (f32[512,128]{1,0:T(8,128)S(1)}, f32[512,128]{1,0:T(8,128)S(1)}, u32[]{:S(2)}, u32[]{:S(2)}) collective-permute-start(f32[512,128]{1,0:T(8,128)S(1)} %collective-permute-done.15.refs_2_), channel_id=1, source_target_pairs={{0,1},{1,0},{2,3},{3,2},{4,5},{5,4},{6,7},{7,6},{8,9},{9,8},{10,11... | collective-permute-start | bytes 786440 | tf_op jit(solution)/shard_map/cond/branch_1_fun/ppermute | solution.py:117
  20.1 0.0 collective-permute-done.14.refs_1_
  20.1 1.5 %collective-permute-done.16.refs_3_ = f32[512,128]{1,0:T(8,128)S(1)} collective-permute-done((f32[512,128]{1,0:T(8,128)S(1)}, f32[512,128]{1,0:T(8,128)S(1)}, u32[]{:S(2)}, u32[]{:S(2)}) %collective-permute-start.16) | collective-permute-done | bytes 262176 | tf_op jit(solution)/shard_map/cond/branch_1_fun/ppermute | solution.py:117
  21.6 2.0 %all-to-all-done.3.refs_4_ = f32[4,512,128]{2,1,0:T(8,128)S(1)} async-done(((f32[4,512,128]{2,1,0:T(8,128)}), f32[4,512,128]{2,1,0:T(8,128)S(1)}, u32[]{:S(2)}, u32[]{:S(2)}) %all-to-all-start.3) | async-done | bytes 1048608 | tf_op jit(solution)/shard_map/cond/branch_1_fun/all_to_all | solution.py:94
  23.6 2.0 %branch_1_fun.2 = f32[4,512,128]{2,1,0:T(8,128)} custom-call(f32[512,128]{1,0:T(8,128)S(1)} %copy-done.3, f32[512,128]{1,0:T(8,128)S(1)} %collective-permute-done.14.refs_1_, f32[512,128]{1,0:T(8,128)S(1)} %collective-permute-done.15.refs_2_, f32[512,128]{1,0:T(8,128)S(1)} %collective-permute-done.16.refs_3_, f32[4,512,128]{2,1,0:T(8,128)S(1)} %all-to-all-done.3.refs_4_), custom_call_target="tpu_custom_call" | custom-call | flops 805306368 | bytes 3145728 | tf_op jit(solution)/shard_map/cond/branch_1_fun/pallas_call | solution.py:53
  25.6 0.0 copy-start.1
  25.6 5.8 %all-to-all-start.4 = ((f32[4,512,128]{2,1,0:T(8,128)}), f32[4,512,128]{2,1,0:T(8,128)S(1)}, u32[]{:S(2)}, u32[]{:S(2)}) async-start(f32[4,512,128]{2,1,0:T(8,128)} %branch_1_fun.2), calls=%async_computation.4 | async-start | bytes 2097152 | tf_op jit(solution)/shard_map/cond/branch_1_fun/all_to_all | solution.py:94
  31.4 0.0 copy-done.1
  31.4 0.1 copy.13
  31.5 5.4 %collective-permute-start.11 = (f32[128,512]{1,0:T(8,128)S(1)}, f32[128,512]{1,0:T(8,128)S(1)}, u32[]{:S(2)}, u32[]{:S(2)}) collective-permute-start(f32[128,512]{1,0:T(8,128)S(1)} %bitcast.37), channel_id=1, source_target_pairs={{0,16},{1,18},{2,17},{3,19},{4,20},{5,22},{6,21},{7,23},{8,52},{9,... | collective-permute-start | bytes 786440 | tf_op jit(solution)/shard_map/cond/branch_1_fun/ppermute | solution.py:118
  37.0 0.7 collective-permute-start.10
  37.7 19.0 %collective-permute-done.11.refs_1_ = f32[128,512]{1,0:T(8,128)S(1)} collective-permute-done((f32[128,512]{1,0:T(8,128)S(1)}, f32[128,512]{1,0:T(8,128)S(1)}, u32[]{:S(2)}, u32[]{:S(2)}) %collective-permute-start.11) | collective-permute-done | bytes 262176 | tf_op jit(solution)/shard_map/cond/branch_1_fun/ppermute | solution.py:118
  56.6 0.0 collective-permute-done.10.refs_0_
  56.7 3.1 %collective-permute-start.12 = (f32[128,512]{1,0:T(8,128)S(1)}, f32[128,512]{1,0:T(8,128)S(1)}, u32[]{:S(2)}, u32[]{:S(2)}) collective-permute-start(f32[128,512]{1,0:T(8,128)S(1)} %get-tuple-element.28), channel_id=1, source_target_pairs={{0,4},{4,0},{8,12},{12,8},{1,5},{5,1},{9,13},{13,9},{2,6},{6,2},{1... | collective-permute-start | bytes 786440 | tf_op jit(solution)/shard_map/cond/branch_1_fun/ppermute | solution.py:125
  59.8 0.0 all-to-all-done.4
  59.8 0.1 fusion.9.refs_4_
  59.8 2.1 %collective-permute-start.18 = (f32[512,128]{1,0:T(8,128)S(1)}, f32[512,128]{1,0:T(8,128)S(1)}, u32[]{:S(2)}, u32[]{:S(2)}) collective-permute-start(f32[512,128]{1,0:T(8,128)S(1)} %fusion.9.refs_4_), channel_id=1, source_target_pairs={{0,2},{2,0},{1,3},{3,1},{4,6},{6,4},{5,7},{7,5},{8,10},{10,8},{9,1... | collective-permute-start | bytes 786440 | tf_op jit(solution)/shard_map/cond/branch_1_fun/ppermute | solution.py:131
  61.9 3.9 %collective-permute-done.12.refs_2_ = f32[128,512]{1,0:T(8,128)S(1)} collective-permute-done((f32[128,512]{1,0:T(8,128)S(1)}, f32[128,512]{1,0:T(8,128)S(1)}, u32[]{:S(2)}, u32[]{:S(2)}) %collective-permute-start.12) | collective-permute-done | bytes 262176 | tf_op jit(solution)/shard_map/cond/branch_1_fun/ppermute | solution.py:125
  65.9 1.9 %collective-permute-start.13 = (f32[2,64,512]{2,1,0:T(8,128)S(1)}, f32[2,64,512]{2,1,0:T(8,128)S(1)}, u32[]{:S(2)}, u32[]{:S(2)}) collective-permute-start(f32[2,64,512]{2,1,0:T(8,128)S(1)} %fusion.7), channel_id=1, source_target_pairs={{0,1},{1,0},{2,3},{3,2},{4,5},{5,4},{6,7},{7,6},{8,9},{9,8},{10,11... | collective-permute-start | bytes 786440 | tf_op jit(solution)/shard_map/cond/branch_1_fun/ppermute | solution.py:128
  67.8 2.4 %collective-permute-start.17 = (f32[512,128]{1,0:T(8,128)S(1)}, f32[512,128]{1,0:T(8,128)S(1)}, u32[]{:S(2)}, u32[]{:S(2)}) collective-permute-start(f32[512,128]{1,0:T(8,128)S(1)} %fusion.9.refs_4_), channel_id=1, source_target_pairs={{0,1},{1,0},{2,3},{3,2},{4,5},{5,4},{6,7},{7,6},{8,9},{9,8},{10,11... | collective-permute-start | bytes 786440 | tf_op jit(solution)/shard_map/cond/branch_1_fun/ppermute | solution.py:132
  70.2 0.0 collective-permute-done.18.refs_6_
  70.2 1.9 %collective-permute-start.19 = (f32[512,128]{1,0:T(8,128)S(1)}, f32[512,128]{1,0:T(8,128)S(1)}, u32[]{:S(2)}, u32[]{:S(2)}) collective-permute-start(f32[512,128]{1,0:T(8,128)S(1)} %collective-permute-done.18.refs_6_), channel_id=1, source_target_pairs={{0,1},{1,0},{2,3},{3,2},{4,5},{5,4},{6,7},{7,6},{8,9},{9,8},{10,11... | collective-permute-start | bytes 786440 | tf_op jit(solution)/shard_map/cond/branch_1_fun/ppermute | solution.py:133
  72.1 0.0 collective-permute-done.13.refs_3_
  72.1 0.0 collective-permute-done.17.refs_5_
  72.2 1.5 %collective-permute-done.19.refs_7_ = f32[512,128]{1,0:T(8,128)S(1)} collective-permute-done((f32[512,128]{1,0:T(8,128)S(1)}, f32[512,128]{1,0:T(8,128)S(1)}, u32[]{:S(2)}, u32[]{:S(2)}) %collective-permute-start.19) | collective-permute-done | bytes 262176 | tf_op jit(solution)/shard_map/cond/branch_1_fun/ppermute | solution.py:133
  73.6 0.6 branch_1_fun.3
  74.2 17.5 %all_to_all.25 = f32[4,64,512]{2,1,0:T(8,128)S(1)} all-to-all(f32[4,64,512]{2,1,0:T(8,128)S(1)} %branch_1_fun.3), channel_id=1, replica_groups=mesh['g'=8,'zl'=2,'xh'=2,'y'=4,'xl'=2,'c'=2] {'y'}, dimensions={0} | all-to-all | bytes 1048576 | tf_op jit(solution)/shard_map/cond/branch_1_fun/all_to_all | solution.py:94
  91.7 0.0 copy-start.4
  91.8 0.6 copy-done.4
  (3 shorter events, 0.1 us)
Async XLA Ops:
  0.0 0.7 copy-start.5
  3.9 4.6 %copy-start.3 = (f32[512,128]{1,0:T(8,128)S(1)}, f32[512,128]{1,0:T(8,128)}, u32[]{:S(2)}) copy-start(f32[512,128]{1,0:T(8,128)} %get-tuple-element.19.refs_0_) | copy-start | bytes 786436 | tf_op jit(solution)/shard_map/cond
  3.9 19.7 %all-to-all-start.3 = ((f32[4,512,128]{2,1,0:T(8,128)}), f32[4,512,128]{2,1,0:T(8,128)S(1)}, u32[]{:S(2)}, u32[]{:S(2)}) async-start(f32[4,512,128]{2,1,0:T(8,128)} %broadcast_in_dim.5), calls=%async_computation.3 | async-start | bytes 2097152 | tf_op jit(solution)/shard_map/cond/branch_1_fun/all_to_all | solution.py:94
  8.5 9.6 %collective-permute-start.15 = (f32[512,128]{1,0:T(8,128)S(1)}, f32[512,128]{1,0:T(8,128)S(1)}, u32[]{:S(2)}, u32[]{:S(2)}) collective-permute-start(f32[512,128]{1,0:T(8,128)S(1)} %copy-done.3), channel_id=1, source_target_pairs={{0,2},{2,0},{1,3},{3,1},{4,6},{6,4},{5,7},{7,5},{8,10},{10,8},{9,1... | collective-permute-start | bytes 786440 | tf_op jit(solution)/shard_map/cond/branch_1_fun/ppermute | solution.py:115
  11.9 8.2 %collective-permute-start.14 = (f32[512,128]{1,0:T(8,128)S(1)}, f32[512,128]{1,0:T(8,128)S(1)}, u32[]{:S(2)}, u32[]{:S(2)}) collective-permute-start(f32[512,128]{1,0:T(8,128)S(1)} %copy-done.3), channel_id=1, source_target_pairs={{0,1},{1,0},{2,3},{3,2},{4,5},{5,4},{6,7},{7,6},{8,9},{9,8},{10,11... | collective-permute-start | bytes 786440 | tf_op jit(solution)/shard_map/cond/branch_1_fun/ppermute | solution.py:116
  18.2 3.4 %collective-permute-start.16 = (f32[512,128]{1,0:T(8,128)S(1)}, f32[512,128]{1,0:T(8,128)S(1)}, u32[]{:S(2)}, u32[]{:S(2)}) collective-permute-start(f32[512,128]{1,0:T(8,128)S(1)} %collective-permute-done.15.refs_2_), channel_id=1, source_target_pairs={{0,1},{1,0},{2,3},{3,2},{4,5},{5,4},{6,7},{7,6},{8,9},{9,8},{10,11... | collective-permute-start | bytes 786440 | tf_op jit(solution)/shard_map/cond/branch_1_fun/ppermute | solution.py:117
  25.6 5.8 %copy-start.1 = (f32[512,128]{1,0:T(8,128)S(1)}, f32[512,128]{1,0:T(8,128)}, u32[]{:S(2)}) copy-start(f32[512,128]{1,0:T(8,128)} %get-tuple-element.23) | copy-start | bytes 786436 | tf_op jit(solution)/shard_map/cond
  25.6 34.2 %all-to-all-start.4 = ((f32[4,512,128]{2,1,0:T(8,128)}), f32[4,512,128]{2,1,0:T(8,128)S(1)}, u32[]{:S(2)}, u32[]{:S(2)}) async-start(f32[4,512,128]{2,1,0:T(8,128)} %branch_1_fun.2), calls=%async_computation.4 | async-start | bytes 2097152 | tf_op jit(solution)/shard_map/cond/branch_1_fun/all_to_all | solution.py:94
  31.5 25.1 %collective-permute-start.11 = (f32[128,512]{1,0:T(8,128)S(1)}, f32[128,512]{1,0:T(8,128)S(1)}, u32[]{:S(2)}, u32[]{:S(2)}) collective-permute-start(f32[128,512]{1,0:T(8,128)S(1)} %bitcast.37), channel_id=1, source_target_pairs={{0,16},{1,18},{2,17},{3,19},{4,20},{5,22},{6,21},{7,23},{8,52},{9,... | collective-permute-start | bytes 786440 | tf_op jit(solution)/shard_map/cond/branch_1_fun/ppermute | solution.py:118
  37.0 19.7 %collective-permute-start.10 = (f32[128,512]{1,0:T(8,128)S(1)}, f32[128,512]{1,0:T(8,128)S(1)}, u32[]{:S(2)}, u32[]{:S(2)}) collective-permute-start(f32[128,512]{1,0:T(8,128)S(1)} %bitcast.38), channel_id=1, source_target_pairs={{0,0},{1,2},{2,1},{3,3},{4,4},{5,6},{6,5},{7,7},{8,36},{9,38},{10,... | collective-permute-start | bytes 786440 | tf_op jit(solution)/shard_map/cond/branch_1_fun/ppermute | solution.py:118
  56.7 9.1 %collective-permute-start.12 = (f32[128,512]{1,0:T(8,128)S(1)}, f32[128,512]{1,0:T(8,128)S(1)}, u32[]{:S(2)}, u32[]{:S(2)}) collective-permute-start(f32[128,512]{1,0:T(8,128)S(1)} %get-tuple-element.28), channel_id=1, source_target_pairs={{0,4},{4,0},{8,12},{12,8},{1,5},{5,1},{9,13},{13,9},{2,6},{6,2},{1... | collective-permute-start | bytes 786440 | tf_op jit(solution)/shard_map/cond/branch_1_fun/ppermute | solution.py:125
  59.8 10.4 %collective-permute-start.18 = (f32[512,128]{1,0:T(8,128)S(1)}, f32[512,128]{1,0:T(8,128)S(1)}, u32[]{:S(2)}, u32[]{:S(2)}) collective-permute-start(f32[512,128]{1,0:T(8,128)S(1)} %fusion.9.refs_4_), channel_id=1, source_target_pairs={{0,2},{2,0},{1,3},{3,1},{4,6},{6,4},{5,7},{7,5},{8,10},{10,8},{9,1... | collective-permute-start | bytes 786440 | tf_op jit(solution)/shard_map/cond/branch_1_fun/ppermute | solution.py:131
  65.9 6.3 %collective-permute-start.13 = (f32[2,64,512]{2,1,0:T(8,128)S(1)}, f32[2,64,512]{2,1,0:T(8,128)S(1)}, u32[]{:S(2)}, u32[]{:S(2)}) collective-permute-start(f32[2,64,512]{2,1,0:T(8,128)S(1)} %fusion.7), channel_id=1, source_target_pairs={{0,1},{1,0},{2,3},{3,2},{4,5},{5,4},{6,7},{7,6},{8,9},{9,8},{10,11... | collective-permute-start | bytes 786440 | tf_op jit(solution)/shard_map/cond/branch_1_fun/ppermute | solution.py:128
  67.8 4.4 %collective-permute-start.17 = (f32[512,128]{1,0:T(8,128)S(1)}, f32[512,128]{1,0:T(8,128)S(1)}, u32[]{:S(2)}, u32[]{:S(2)}) collective-permute-start(f32[512,128]{1,0:T(8,128)S(1)} %fusion.9.refs_4_), channel_id=1, source_target_pairs={{0,1},{1,0},{2,3},{3,2},{4,5},{5,4},{6,7},{7,6},{8,9},{9,8},{10,11... | collective-permute-start | bytes 786440 | tf_op jit(solution)/shard_map/cond/branch_1_fun/ppermute | solution.py:132
  70.2 3.4 %collective-permute-start.19 = (f32[512,128]{1,0:T(8,128)S(1)}, f32[512,128]{1,0:T(8,128)S(1)}, u32[]{:S(2)}, u32[]{:S(2)}) collective-permute-start(f32[512,128]{1,0:T(8,128)S(1)} %collective-permute-done.18.refs_6_), channel_id=1, source_target_pairs={{0,1},{1,0},{2,3},{3,2},{4,5},{5,4},{6,7},{7,6},{8,9},{9,8},{10,11... | collective-permute-start | bytes 786440 | tf_op jit(solution)/shard_map/cond/branch_1_fun/ppermute | solution.py:133
  91.7 0.7 copy-start.4

commit v5 on v4

--- a/solution.py
+++ b/solution.py
@@ -109,9 +109,31 @@
 FLIP = [(0, 1), (1, 0)]
 
 
-def branch(swap, moments, basis):
-    basis_y = exchange(jnp.broadcast_to(basis, (4, 512, 128)), "y")
-    turned = basis.T
+def spread_kernel(slot_ref, v_ref, spread_ref, turned_ref, swap_ref):
+    swap_ref[0] = slot_ref[at("g")]
+    value = v_ref[...]
+    for place in range(4):
+        spread_ref[place] = value
+    turned_ref[...] = value.T
+
+
+def spread_out(slot_order, v):
+    return pl.pallas_call(
+        spread_kernel,
+        out_shape=(
+            jax.ShapeDtypeStruct((4, 512, 128), jnp.float32),
+            jax.ShapeDtypeStruct((128, 512), jnp.float32),
+            jax.ShapeDtypeStruct((1,), jnp.int32),
+        ),
+        in_specs=[IN_SMEM, IN_VMEM],
+        out_specs=(IN_VMEM, IN_VMEM, IN_SMEM),
+        compiler_params=SMALL,
+        cost_estimate=pl.CostEstimate(flops=2**20, bytes_accessed=2**21, transcendentals=0),
+    )(slot_order, v)
+
+
+def branch(swap, moments, spread, turned):
+    basis_y = exchange(spread, "y")
     by_x = lax.ppermute(moments, "xl", FLIP)
     by_c = lax.ppermute(moments, "c", FLIP)
     by_xc = lax.ppermute(by_x, "c", FLIP)
@@ -131,13 +153,13 @@
     z_x = lax.ppermute(total, "xl", FLIP)
     z_c = lax.ppermute(total, "c", FLIP)
     z_xc = lax.ppermute(z_x, "c", FLIP)
-    out = exchange(project(swap, kept, other, mixed, (total, z_c, z_x, z_xc)), "y")
-    return ((out[0] + out[1]) + (out[2] + out[3])).T
+    return exchange(project(swap, kept, other, mixed, (total, z_c, z_x, z_xc)), "y")
 
 
 def body(moments, basis, slot_order):
-    swap = lax.dynamic_index_in_dim(slot_order, lax.axis_index("g"), 0, keepdims=False)
-    return lax.cond(swap == 0, functools.partial(branch, 0), functools.partial(branch, 1), moments, basis)
+    spread, turned, swap = spread_out(slot_order, basis)
+    out = lax.switch(swap[0], (functools.partial(branch, 0), functools.partial(branch, 1)), moments, spread, turned)
+    return ((out[0] + out[1]) + (out[2] + out[3])).T
 
 
 def solution(mesh):

time: 93 us -> 92.7 us (level)
  local copies, waits for them, and re-layouts: 4.01 us -> 1.61 us
  Pallas kernels: 2.62 us -> 4.2 us
    broadcast_in_dim x1 -> x0, local copies, waits for them, and re-layouts: 1.99 us -> none  [branch(): basis_y = exchange(jnp.broadcast_to(basis, (4, 512, 128)), 'y')]
    pallas_call x0 -> x1, Pallas kernels: none -> 1.59 us  [spread_out(): pl.pallas_call(spread_kernel, out_shape=(jax.ShapeDtypeStruct((4, 512, 12...]
where the time goes in v5:
time: 92.7 us; the launch traced here: 92.1 us
  starting transfers between devices  34.8 us (38%)
  waiting for transfers between devices  32.3 us (35%)
  blocking collectives  17.5 us (19%)
  Pallas kernels  4.2 us (5%)
  local copies, waits for them, and re-layouts  1.61 us (2%)
    ppermute x2, waiting for transfers between devices, branch(): lax.ppermute(turned, (*ROW, *COL), turning(swap, m))  19.1 us
    all_to_all x1, blocking collectives, exchange(): return lax.all_to_all(x, axes, 0, 0, tiled=True)  17.5 us
    all_to_all x2, starting transfers between devices, exchange(): return lax.all_to_all(x, axes, 0, 0, tiled=True)  10.1 us
    ppermute x2, starting transfers between devices, branch(): lax.ppermute(turned, (*ROW, *COL), turning(swap, m))  6.1 us
    ppermute x1, waiting for transfers between devices, branch(): by_x = lax.ppermute(moments, 'xl', FLIP)  4.32 us
    ppermute x1, waiting for transfers between devices, branch(): other = lax.ppermute(away, 'y', [(y, y ^ 1) for y in range(4)])  3.9 us
    ppermute x1, starting transfers between devices, branch(): by_x = lax.ppermute(moments, 'xl', FLIP)  3.39 us
    ppermute x1, starting transfers between devices, branch(): other = lax.ppermute(away, 'y', [(y, y ^ 1) for y in range(4)])  3.06 us
  transfers between devices with their start and end apart: 12, of which 6 were waited for; matrix products, arithmetic and copies ran while one was open for 0% of the time, Pallas kernels for 0%

profile of v5, /device:TPU:192, one launch (start us, length us, event | category | flops | bytes accessed | tf_op | source)
XLA Modules:
  0.0 92.1 jit_solution(3595877711036568447)
XLA Ops:
  0.0 0.0 copy-start
  0.0 0.9 %copy-done = f32[512,128]{1,0:T(8,128)S(1)} copy-done((f32[512,128]{1,0:T(8,128)S(1)}, f32[512,128]{1,0:T(8,128)}, u32[]{:S(2)}) %copy-start) | copy-done | bytes 262168
  1.0 0.0 copy-start.1
  1.0 0.7 copy-done.1
  1.6 0.0 copy-start.2
  1.6 1.6 %shard_map.37 = (f32[4,512,128]{2,1,0:T(8,128)}, f32[128,512]{1,0:T(8,128)S(1)}, s32[1]{0:T(128)}) custom-call(s32[8]{0:T(128)S(1)} %copy-done.1, f32[512,128]{1,0:T(8,128)S(1)} %copy-done), custom_call_target="tpu_custom_call" | custom-call | flops 1048576 | bytes 2097152 | tf_op jit(solution)/shard_map/pallas_call | solution.py:121
  3.9 0.0 copy-done.2
  3.9 87.5 %conditional.1 = (f32[4,64,512]{2,1,0:T(8,128)S(1)}) conditional(s32[]{:T(128)} %bitcast.16, (f32[128,512]{1,0:T(8,128)S(1)}, f32[512,128]{1,0:T(8,128)S(1)}, f32[4,512,128]{2,1,0:T(8,128)}) %tuple.16, (f32[128,512]{1,0:T(8,128)S(1)}, f32[512,128]{1,0:T(8,128)S(1)}, f32[4,512,128]{2,1,0:T(8,128)}) %tuple.17), branch_computations={%region_0.1_spmd, %region_1.2_spmd} | conditional | flops 1208352768 | bytes 26215136 | solution.py:161
  3.9 4.5 %all-to-all-start = ((f32[4,512,128]{2,1,0:T(8,128)}), f32[4,512,128]{2,1,0:T(8,128)S(1)}, u32[]{:S(2)}, u32[]{:S(2)}) async-start(f32[4,512,128]{2,1,0:T(8,128)} %get-tuple-element.22), calls=%async_computation | async-start | bytes 2097152 | tf_op jit(solution)/shard_map/cond/branch_0_fun/all_to_all | solution.py:94
  8.4 3.4 %collective-permute-start.5 = (f32[512,128]{1,0:T(8,128)S(1)}, f32[512,128]{1,0:T(8,128)S(1)}, u32[]{:S(2)}, u32[]{:S(2)}) collective-permute-start(f32[512,128]{1,0:T(8,128)S(1)} %get-tuple-element.21.refs_0_), channel_id=1, source_target_pairs={{0,2},{2,0},{1,3},{3,1},{4,6},{6,4},{5,7},{7,5},{8,10},{10,8},{9,1... | collective-permute-start | bytes 786440 | tf_op jit(solution)/shard_map/cond/branch_0_fun/ppermute | solution.py:137
  11.8 1.9 %collective-permute-start.4 = (f32[512,128]{1,0:T(8,128)S(1)}, f32[512,128]{1,0:T(8,128)S(1)}, u32[]{:S(2)}, u32[]{:S(2)}) collective-permute-start(f32[512,128]{1,0:T(8,128)S(1)} %get-tuple-element.21.refs_0_), channel_id=1, source_target_pairs={{0,1},{1,0},{2,3},{3,2},{4,5},{5,4},{6,7},{7,6},{8,9},{9,8},{10,11... | collective-permute-start | bytes 786440 | tf_op jit(solution)/shard_map/cond/branch_0_fun/ppermute | solution.py:138
  13.7 4.3 %collective-permute-done.5.refs_2_ = f32[512,128]{1,0:T(8,128)S(1)} collective-permute-done((f32[512,128]{1,0:T(8,128)S(1)}, f32[512,128]{1,0:T(8,128)S(1)}, u32[]{:S(2)}, u32[]{:S(2)}) %collective-permute-start.5) | collective-permute-done | bytes 262176 | tf_op jit(solution)/shard_map/cond/branch_0_fun/ppermute | solution.py:137
  18.0 1.9 %collective-permute-start.6 = (f32[512,128]{1,0:T(8,128)S(1)}, f32[512,128]{1,0:T(8,128)S(1)}, u32[]{:S(2)}, u32[]{:S(2)}) collective-permute-start(f32[512,128]{1,0:T(8,128)S(1)} %collective-permute-done.5.refs_2_), channel_id=1, source_target_pairs={{0,1},{1,0},{2,3},{3,2},{4,5},{5,4},{6,7},{7,6},{8,9},{9,8},{10,11... | collective-permute-start | bytes 786440 | tf_op jit(solution)/shard_map/cond/branch_0_fun/ppermute | solution.py:139
  19.9 0.0 collective-permute-done.4.refs_1_
  19.9 1.5 %collective-permute-done.6.refs_3_ = f32[512,128]{1,0:T(8,128)S(1)} collective-permute-done((f32[512,128]{1,0:T(8,128)S(1)}, f32[512,128]{1,0:T(8,128)S(1)}, u32[]{:S(2)}, u32[]{:S(2)}) %collective-permute-start.6) | collective-permute-done | bytes 262176 | tf_op jit(solution)/shard_map/cond/branch_0_fun/ppermute | solution.py:139
  21.4 2.0 %all-to-all-done.refs_4_ = f32[4,512,128]{2,1,0:T(8,128)S(1)} async-done(((f32[4,512,128]{2,1,0:T(8,128)}), f32[4,512,128]{2,1,0:T(8,128)S(1)}, u32[]{:S(2)}, u32[]{:S(2)}) %all-to-all-start) | async-done | bytes 1048608 | tf_op jit(solution)/shard_map/cond/branch_0_fun/all_to_all | solution.py:94
  23.5 2.0 %branch_0_fun.2 = f32[4,512,128]{2,1,0:T(8,128)} custom-call(f32[512,128]{1,0:T(8,128)S(1)} %get-tuple-element.21.refs_0_, f32[512,128]{1,0:T(8,128)S(1)} %collective-permute-done.4.refs_1_, f32[512,128]{1,0:T(8,128)S(1)} %collective-permute-done.5.refs_2_, f32[512,128]{1,0:T(8,128)S(1)} %collective-permute-done.6.refs_3_, ...), custom_call_target="tpu_custom_call" | custom-call | flops 805306368 | bytes 3145728 | tf_op jit(solution)/shard_map/cond/branch_0_fun/pallas_call | solution.py:53
  25.5 5.6 %all-to-all-start.1 = ((f32[4,512,128]{2,1,0:T(8,128)}), f32[4,512,128]{2,1,0:T(8,128)S(1)}, u32[]{:S(2)}, u32[]{:S(2)}) async-start(f32[4,512,128]{2,1,0:T(8,128)} %branch_0_fun.2), calls=%async_computation.1 | async-start | bytes 2097152 | tf_op jit(solution)/shard_map/cond/branch_0_fun/all_to_all | solution.py:94
  31.1 5.4 %collective-permute-start.1 = (f32[128,512]{1,0:T(8,128)S(1)}, f32[128,512]{1,0:T(8,128)S(1)}, u32[]{:S(2)}, u32[]{:S(2)}) collective-permute-start(f32[128,512]{1,0:T(8,128)S(1)} %get-tuple-element.20), channel_id=1, source_target_pairs={{0,16},{1,18},{2,17},{3,19},{4,20},{5,22},{6,21},{7,23},{8,52},{9,... | collective-permute-start | bytes 786440 | tf_op jit(solution)/shard_map/cond/branch_0_fun/ppermute | solution.py:140
  36.5 0.7 collective-permute-start
  37.2 19.1 %collective-permute-done.1.refs_1_ = f32[128,512]{1,0:T(8,128)S(1)} collective-permute-done((f32[128,512]{1,0:T(8,128)S(1)}, f32[128,512]{1,0:T(8,128)S(1)}, u32[]{:S(2)}, u32[]{:S(2)}) %collective-permute-start.1) | collective-permute-done | bytes 262176 | tf_op jit(solution)/shard_map/cond/branch_0_fun/ppermute | solution.py:140
  56.3 0.0 collective-permute-done.refs_0_
  56.4 3.1 %collective-permute-start.2 = (f32[128,512]{1,0:T(8,128)S(1)}, f32[128,512]{1,0:T(8,128)S(1)}, u32[]{:S(2)}, u32[]{:S(2)}) collective-permute-start(f32[128,512]{1,0:T(8,128)S(1)} %get-tuple-element.33), channel_id=1, source_target_pairs={{0,4},{4,0},{8,12},{12,8},{1,5},{5,1},{9,13},{13,9},{2,6},{6,2},{1... | collective-permute-start | bytes 786440 | tf_op jit(solution)/shard_map/cond/branch_0_fun/ppermute | solution.py:147
  59.5 0.0 all-to-all-done.1
  59.5 0.1 fusion.3.refs_4_
  59.5 2.1 %collective-permute-start.8 = (f32[512,128]{1,0:T(8,128)S(1)}, f32[512,128]{1,0:T(8,128)S(1)}, u32[]{:S(2)}, u32[]{:S(2)}) collective-permute-start(f32[512,128]{1,0:T(8,128)S(1)} %fusion.3.refs_4_), channel_id=1, source_target_pairs={{0,2},{2,0},{1,3},{3,1},{4,6},{6,4},{5,7},{7,5},{8,10},{10,8},{9,1... | collective-permute-start | bytes 786440 | tf_op jit(solution)/shard_map/cond/branch_0_fun/ppermute | solution.py:153
  61.6 3.9 %collective-permute-done.2.refs_2_ = f32[128,512]{1,0:T(8,128)S(1)} collective-permute-done((f32[128,512]{1,0:T(8,128)S(1)}, f32[128,512]{1,0:T(8,128)S(1)}, u32[]{:S(2)}, u32[]{:S(2)}) %collective-permute-start.2) | collective-permute-done | bytes 262176 | tf_op jit(solution)/shard_map/cond/branch_0_fun/ppermute | solution.py:147
  65.6 1.9 %collective-permute-start.3 = (f32[2,64,512]{2,1,0:T(8,128)S(1)}, f32[2,64,512]{2,1,0:T(8,128)S(1)}, u32[]{:S(2)}, u32[]{:S(2)}) collective-permute-start(f32[2,64,512]{2,1,0:T(8,128)S(1)} %fusion.1), channel_id=1, source_target_pairs={{0,1},{1,0},{2,3},{3,2},{4,5},{5,4},{6,7},{7,6},{8,9},{9,8},{10,11... | collective-permute-start | bytes 786440 | tf_op jit(solution)/shard_map/cond/branch_0_fun/ppermute | solution.py:150
  67.5 2.4 %collective-permute-start.7 = (f32[512,128]{1,0:T(8,128)S(1)}, f32[512,128]{1,0:T(8,128)S(1)}, u32[]{:S(2)}, u32[]{:S(2)}) collective-permute-start(f32[512,128]{1,0:T(8,128)S(1)} %fusion.3.refs_4_), channel_id=1, source_target_pairs={{0,1},{1,0},{2,3},{3,2},{4,5},{5,4},{6,7},{7,6},{8,9},{9,8},{10,11... | collective-permute-start | bytes 786440 | tf_op jit(solution)/shard_map/cond/branch_0_fun/ppermute | solution.py:154
  69.9 0.0 collective-permute-done.8.refs_6_
  69.9 1.9 %collective-permute-start.9 = (f32[512,128]{1,0:T(8,128)S(1)}, f32[512,128]{1,0:T(8,128)S(1)}, u32[]{:S(2)}, u32[]{:S(2)}) collective-permute-start(f32[512,128]{1,0:T(8,128)S(1)} %collective-permute-done.8.refs_6_), channel_id=1, source_target_pairs={{0,1},{1,0},{2,3},{3,2},{4,5},{5,4},{6,7},{7,6},{8,9},{9,8},{10,11... | collective-permute-start | bytes 786440 | tf_op jit(solution)/shard_map/cond/branch_0_fun/ppermute | solution.py:155
  71.8 0.0 collective-permute-done.3.refs_3_
  71.9 0.0 collective-permute-done.7.refs_5_
  71.9 1.5 %collective-permute-done.9.refs_7_ = f32[512,128]{1,0:T(8,128)S(1)} collective-permute-done((f32[512,128]{1,0:T(8,128)S(1)}, f32[512,128]{1,0:T(8,128)S(1)}, u32[]{:S(2)}, u32[]{:S(2)}) %collective-permute-start.9) | collective-permute-done | bytes 262176 | tf_op jit(solution)/shard_map/cond/branch_0_fun/ppermute | solution.py:155
  73.3 0.6 branch_0_fun.3
  73.9 17.5 %all_to_all.24 = f32[4,64,512]{2,1,0:T(8,128)S(1)} all-to-all(f32[4,64,512]{2,1,0:T(8,128)S(1)} %branch_0_fun.3), channel_id=1, replica_groups=mesh['g'=8,'zl'=2,'xh'=2,'y'=4,'xl'=2,'c'=2] {'y'}, dimensions={0} | all-to-all | bytes 1048576 | tf_op jit(solution)/shard_map/cond/branch_0_fun/all_to_all | solution.py:94
  91.4 0.7 fusion.9
  (2 shorter events, 0.1 us)
Async XLA Ops:
  0.0 0.9 %copy-start = (f32[512,128]{1,0:T(8,128)S(1)}, f32[512,128]{1,0:T(8,128)}, u32[]{:S(2)}) copy-start(f32[512,128]{1,0:T(8,128)} %v_ref.1) | copy-start | bytes 786436
  1.0 0.7 copy-start.1
  1.6 2.3 %copy-start.2 = (f32[512,128]{1,0:T(8,128)S(1)}, f32[512,128]{1,0:T(8,128)}, u32[]{:S(2)}) copy-start(f32[512,128]{1,0:T(8,128)} %param.5) | copy-start | bytes 786436
  3.9 19.6 %all-to-all-start = ((f32[4,512,128]{2,1,0:T(8,128)}), f32[4,512,128]{2,1,0:T(8,128)S(1)}, u32[]{:S(2)}, u32[]{:S(2)}) async-start(f32[4,512,128]{2,1,0:T(8,128)} %get-tuple-element.22), calls=%async_computation | async-start | bytes 2097152 | tf_op jit(solution)/shard_map/cond/branch_0_fun/all_to_all | solution.py:94
  8.4 9.6 %collective-permute-start.5 = (f32[512,128]{1,0:T(8,128)S(1)}, f32[512,128]{1,0:T(8,128)S(1)}, u32[]{:S(2)}, u32[]{:S(2)}) collective-permute-start(f32[512,128]{1,0:T(8,128)S(1)} %get-tuple-element.21.refs_0_), channel_id=1, source_target_pairs={{0,2},{2,0},{1,3},{3,1},{4,6},{6,4},{5,7},{7,5},{8,10},{10,8},{9,1... | collective-permute-start | bytes 786440 | tf_op jit(solution)/shard_map/cond/branch_0_fun/ppermute | solution.py:137
  11.8 8.2 %collective-permute-start.4 = (f32[512,128]{1,0:T(8,128)S(1)}, f32[512,128]{1,0:T(8,128)S(1)}, u32[]{:S(2)}, u32[]{:S(2)}) collective-permute-start(f32[512,128]{1,0:T(8,128)S(1)} %get-tuple-element.21.refs_0_), channel_id=1, source_target_pairs={{0,1},{1,0},{2,3},{3,2},{4,5},{5,4},{6,7},{7,6},{8,9},{9,8},{10,11... | collective-permute-start | bytes 786440 | tf_op jit(solution)/shard_map/cond/branch_0_fun/ppermute | solution.py:138
  18.0 3.4 %collective-permute-start.6 = (f32[512,128]{1,0:T(8,128)S(1)}, f32[512,128]{1,0:T(8,128)S(1)}, u32[]{:S(2)}, u32[]{:S(2)}) collective-permute-start(f32[512,128]{1,0:T(8,128)S(1)} %collective-permute-done.5.refs_2_), channel_id=1, source_target_pairs={{0,1},{1,0},{2,3},{3,2},{4,5},{5,4},{6,7},{7,6},{8,9},{9,8},{10,11... | collective-permute-start | bytes 786440 | tf_op jit(solution)/shard_map/cond/branch_0_fun/ppermute | solution.py:139
  25.5 34.0 %all-to-all-start.1 = ((f32[4,512,128]{2,1,0:T(8,128)}), f32[4,512,128]{2,1,0:T(8,128)S(1)}, u32[]{:S(2)}, u32[]{:S(2)}) async-start(f32[4,512,128]{2,1,0:T(8,128)} %branch_0_fun.2), calls=%async_computation.1 | async-start | bytes 2097152 | tf_op jit(solution)/shard_map/cond/branch_0_fun/all_to_all | solution.py:94
  31.1 25.2 %collective-permute-start.1 = (f32[128,512]{1,0:T(8,128)S(1)}, f32[128,512]{1,0:T(8,128)S(1)}, u32[]{:S(2)}, u32[]{:S(2)}) collective-permute-start(f32[128,512]{1,0:T(8,128)S(1)} %get-tuple-element.20), channel_id=1, source_target_pairs={{0,16},{1,18},{2,17},{3,19},{4,20},{5,22},{6,21},{7,23},{8,52},{9,... | collective-permute-start | bytes 786440 | tf_op jit(solution)/shard_map/cond/branch_0_fun/ppermute | solution.py:140
  36.5 19.8 %collective-permute-start = (f32[128,512]{1,0:T(8,128)S(1)}, f32[128,512]{1,0:T(8,128)S(1)}, u32[]{:S(2)}, u32[]{:S(2)}) collective-permute-start(f32[128,512]{1,0:T(8,128)S(1)} %get-tuple-element.20), channel_id=1, source_target_pairs={{0,0},{1,2},{2,1},{3,3},{4,4},{5,6},{6,5},{7,7},{8,36},{9,38},{10,... | collective-permute-start | bytes 786440 | tf_op jit(solution)/shard_map/cond/branch_0_fun/ppermute | solution.py:140
  56.4 9.1 %collective-permute-start.2 = (f32[128,512]{1,0:T(8,128)S(1)}, f32[128,512]{1,0:T(8,128)S(1)}, u32[]{:S(2)}, u32[]{:S(2)}) collective-permute-start(f32[128,512]{1,0:T(8,128)S(1)} %get-tuple-element.33), channel_id=1, source_target_pairs={{0,4},{4,0},{8,12},{12,8},{1,5},{5,1},{9,13},{13,9},{2,6},{6,2},{1... | collective-permute-start | bytes 786440 | tf_op jit(solution)/shard_map/cond/branch_0_fun/ppermute | solution.py:147
  59.5 10.4 %collective-permute-start.8 = (f32[512,128]{1,0:T(8,128)S(1)}, f32[512,128]{1,0:T(8,128)S(1)}, u32[]{:S(2)}, u32[]{:S(2)}) collective-permute-start(f32[512,128]{1,0:T(8,128)S(1)} %fusion.3.refs_4_), channel_id=1, source_target_pairs={{0,2},{2,0},{1,3},{3,1},{4,6},{6,4},{5,7},{7,5},{8,10},{10,8},{9,1... | collective-permute-start | bytes 786440 | tf_op jit(solution)/shard_map/cond/branch_0_fun/ppermute | solution.py:153
  65.6 6.3 %collective-permute-start.3 = (f32[2,64,512]{2,1,0:T(8,128)S(1)}, f32[2,64,512]{2,1,0:T(8,128)S(1)}, u32[]{:S(2)}, u32[]{:S(2)}) collective-permute-start(f32[2,64,512]{2,1,0:T(8,128)S(1)} %fusion.1), channel_id=1, source_target_pairs={{0,1},{1,0},{2,3},{3,2},{4,5},{5,4},{6,7},{7,6},{8,9},{9,8},{10,11... | collective-permute-start | bytes 786440 | tf_op jit(solution)/shard_map/cond/branch_0_fun/ppermute | solution.py:150
  67.5 4.4 %collective-permute-start.7 = (f32[512,128]{1,0:T(8,128)S(1)}, f32[512,128]{1,0:T(8,128)S(1)}, u32[]{:S(2)}, u32[]{:S(2)}) collective-permute-start(f32[512,128]{1,0:T(8,128)S(1)} %fusion.3.refs_4_), channel_id=1, source_target_pairs={{0,1},{1,0},{2,3},{3,2},{4,5},{5,4},{6,7},{7,6},{8,9},{9,8},{10,11... | collective-permute-start | bytes 786440 | tf_op jit(solution)/shard_map/cond/branch_0_fun/ppermute | solution.py:154
  69.9 3.4 %collective-permute-start.9 = (f32[512,128]{1,0:T(8,128)S(1)}, f32[512,128]{1,0:T(8,128)S(1)}, u32[]{:S(2)}, u32[]{:S(2)}) collective-permute-start(f32[512,128]{1,0:T(8,128)S(1)} %collective-permute-done.8.refs_6_), channel_id=1, source_target_pairs={{0,1},{1,0},{2,3},{3,2},{4,5},{5,4},{6,7},{7,6},{8,9},{9,8},{10,11... | collective-permute-start | bytes 786440 | tf_op jit(solution)/shard_map/cond/branch_0_fun/ppermute | solution.py:155
